TPU v7x, 512 devices: a whole 4x8x8 slice. The times are simulated.
512 devices in a mesh: gx: 4 (over y_hi), gy: 16 (over z, y_lo), gz: 8 (over x, core).
Axes of the slice: x: 4, y: 8 (y_hi: 4, y_lo: 2; y = y_hi * 2 + y_lo), z: 8, core: 2. Of those that a mesh axis runs over, the one named last changes fastest.
Arguments:
- nodal_scalar_values: float32 [3, 32, 128, 16384], P(None, 'gx', 'gy', 'gz'), may hold values from -6 to 6
- geometry: float32 [6, 4, 16, 2048], P(None, 'gx', 'gy', 'gz'), may hold values from -1.2 to 4, as said below
Outputs:
- assembled: float32 [3, 32, 128, 16384], P(None, 'gx', 'gy', 'gz')
Inputs may be any that keep to these rules, and one draw needn't show every extreme that they name: `geometry`: G00, G11 and G22 are positive; each off-diagonal factor is at most 0.3 times the root of the product of its two diagonal factors in magnitude.
All inputs are finite; a program needn't handle non-finite values.
Results may differ from a plain program's by a relative error of at most 0.00007.
Values sent between devices are 32-bit elements; how exact they have to be, the bound alone decides.
A program may use at most 64 MiB of HBM per device.

v0:
```python
import math

import jax
import jax.numpy as jnp
import numpy as np
from jax import lax
from jax.sharding import PartitionSpec as P

interior_points = [
    -0.8717401485096066,
    -0.5917001814331423,
    -0.2092992179024789,
    0.2092992179024789,
    0.5917001814331423,
    0.8717401485096066,
]


def shifted(array, axis, by):
    count = lax.axis_size(axis)
    pairs = [(i, i + by) for i in range(count) if 0 <= i + by < count]
    return lax.ppermute(array, axis, pairs)


def legendre_seven(point):
    previous = 1.0
    current = point
    for order in range(1, 7):
        following = ((2 * order + 1) * point * current - order * previous) / (order + 1)
        previous = current
        current = following
    return current


def gll_tables():
    degree = 7
    points = [-1.0] + interior_points + [1.0]
    values = [legendre_seven(point) for point in points]
    node_count = degree + 1
    weights = np.array([2.0 / (degree * (degree + 1) * value * value) for value in values])
    derivative = np.zeros((node_count, node_count))
    for row_index in range(node_count):
        for col_index in range(node_count):
            if row_index != col_index:
                derivative[row_index, col_index] = values[row_index] / (
                    values[col_index] * (points[row_index] - points[col_index])
                )
    derivative[0, 0] = -degree * (degree + 1) / 4.0
    derivative[node_count - 1, node_count - 1] = degree * (degree + 1) / 4.0
    return (derivative, weights)


def apply_axis(field_in, matrix, direction):
    length = field_in.shape[direction]
    block_size = math.gcd(length, 128)
    big_table = jnp.kron(jnp.eye(block_size // 8, dtype=jnp.float32), matrix)
    dim_list = list(field_in.shape)
    folded_shape = (
        dim_list[:direction] + [length // block_size, block_size] + dim_list[direction + 1 :]
    )
    folded_field = field_in.reshape(folded_shape)
    patterns = ["nbyz,ab->nayz", "xnbz,ab->xnaz", "xynb,ab->xyna"]
    result = jnp.einsum(
        patterns[direction], folded_field, big_table, precision=lax.Precision.HIGHEST
    )
    return result.reshape(field_in.shape)


def expand(field_component, target):
    elem_x, elem_y, elem_z = field_component.shape
    spread = jnp.broadcast_to(
        field_component[:, None, :, None, :, None], (elem_x, 8, elem_y, 8, elem_z, 8)
    )
    return spread.reshape(target)


def stiffness(field_in, geometry):
    derivative, weights = gll_tables()
    matrix = jnp.asarray(derivative, jnp.float32)
    weight_row = jnp.asarray(weights, jnp.float32)
    size_x, size_y, size_z = field_in.shape
    weight_x = jnp.tile(weight_row, size_x // 8)
    weight_y = jnp.tile(weight_row, size_y // 8)
    weight_z = jnp.tile(weight_row, size_z // 8)
    node_weight = weight_x[:, None, None] * weight_y[None, :, None] * weight_z[None, None, :]
    grad_x = apply_axis(field_in, matrix, 0)
    grad_y = apply_axis(field_in, matrix, 1)
    grad_z = apply_axis(field_in, matrix, 2)
    factors = [expand(geometry[index], field_in.shape) for index in range(6)]
    flux_x = node_weight * (factors[0] * grad_x + factors[3] * grad_y + factors[4] * grad_z)
    flux_y = node_weight * (factors[3] * grad_x + factors[1] * grad_y + factors[5] * grad_z)
    flux_z = node_weight * (factors[4] * grad_x + factors[5] * grad_y + factors[2] * grad_z)
    transposed = matrix.T
    return (
        apply_axis(flux_x, transposed, 0)
        + apply_axis(flux_y, transposed, 1)
        + apply_axis(flux_z, transposed, 2)
    )


def combine(middle, below_plane, above_plane, direction):
    length = middle.shape[direction]
    from_above = jnp.concatenate(
        [lax.slice_in_dim(middle, 1, length, axis=direction), above_plane], axis=direction
    )
    from_below = jnp.concatenate(
        [below_plane, lax.slice_in_dim(middle, 0, length - 1, axis=direction)], axis=direction
    )
    position = lax.broadcasted_iota(jnp.int32, middle.shape, direction) % 8
    return (
        middle
        + jnp.where(position == 7, from_above, 0.0)
        + jnp.where(position == 0, from_below, 0.0)
    )


def edge_planes(summed, direction):
    length = summed.shape[direction]
    first_plane = lax.slice_in_dim(summed, 0, 1, axis=direction)
    last_plane = lax.slice_in_dim(summed, length - 1, length, axis=direction)
    return (first_plane, last_plane)


def local(nodal_scalar_values, geometry):
    component_count = nodal_scalar_values.shape[0]
    local_terms = jnp.stack(
        [
            stiffness(nodal_scalar_values[component], geometry)
            for component in range(component_count)
        ]
    )
    summed = local_terms
    first_plane, last_plane = edge_planes(summed, 1)
    below_plane = shifted(last_plane, "gx", 1)
    above_plane = shifted(first_plane, "gx", -1)
    summed = combine(summed, below_plane, above_plane, 1)
    first_plane, last_plane = edge_planes(summed, 2)
    below_plane = shifted(last_plane, "gy", 1)
    above_plane = shifted(first_plane, "gy", -1)
    summed = combine(summed, below_plane, above_plane, 2)
    first_plane, last_plane = edge_planes(summed, 3)
    below_plane = shifted(last_plane, "gz", 1)
    above_plane = shifted(first_plane, "gz", -1)
    summed = combine(summed, below_plane, above_plane, 3)
    return summed


def solution(mesh):
    return jax.shard_map(
        local,
        mesh=mesh,
        in_specs=(P(None, "gx", "gy", "gz"), P(None, "gx", "gy", "gz")),
        out_specs=P(None, "gx", "gy", "gz"),
        check_vma=False,
    )
```

profile of v0, /device:TPU:442, one launch (start us, length us, event | category | flops | bytes accessed | tf_op | source)
XLA Modules:
  0.0 80.4 jit_solution(14125740864815316012)
XLA Ops:
  0.0 1.6 %fusion.134 = (f32[1,8,8,2048]{3,2,1,0:T(8,128)S(1)}, f32[1,8,8,2048]{3,2,1,0:T(8,128)S(1)}, f32[1,8,8,2048]{3,2,1,0:T(8,128)S(1)}) fusion(f32[3,8,8,2048]{3,2,1,0:T(8,128)} %param.8), kind=kLoop, calls=%fused_computation.185 | loop fusion | bytes 3145728 | tf_op jit(solution)/shard_map/slice | solution.py:128
  1.6 0.3 copy-done.4
  1.9 0.6 fusion.18
  2.5 0.6 fusion.22
  3.0 0.6 fusion.20
  3.6 0.8 %fusion.32 = f32[8,8,2048]{2,0,1:T(8,128)S(1)} fusion(f32[8,8,1]{1,0,2:T(8,128)S(1)} %copy-done.12, f32[1,8,8,2048]{3,2,1,0:T(8,128)S(1)} %get-tuple-element.19), kind=kOutput, calls=%fused_computation.64 | convolution fusion | flops 12582912 | bytes 1048832 | tf_op jit(solution)/shard_map/nbyz,ab->nayz/dot_general | solution.py:63
  4.4 1.6 %copy_bitcast_fusion = (f32[8,8,16,128]{3,0,2,1:T(8,128)}, f32[8,8,16,128]{3,0,2,1:T(8,128)}) fusion(f32[1,8,8,2048]{3,2,1,0:T(8,128)S(1)} %get-tuple-element.19, f32[1,8,8,2048]{3,2,1,0:T(8,128)S(1)} %get-tuple-element.18), kind=kLoop, calls=%fused_computation.111 | loop fusion | bytes 2097152 | tf_op jit(solution)/shard_map/reshape;squeeze | solution.py:61
  6.1 0.8 fusion.42
  6.9 1.5 %broadcast_multiply_fusion = (f32[16,8,16,8]{3,2,1,0:T(8,128)}, f32[16,8,16,8]{3,2,1,0:T(8,128)}) fusion(f32[8,8]{1,0:T(8,128)S(1)} %copy-done.15, f32[16,16]{1,0:T(8,128)S(1)} %fusion.123, f32[8,8]{1,0:T(8,128)S(1)} %copy-done.16), kind=kLoop, calls=%fused_computation.107 | loop fusion | flops 32768 | bytes 132608 | tf_op jit(solution)/shard_map/jit(kron)/mul | solution.py:56
  8.4 1.6 %reshape.403 = f32[128,128,1,1]{1,0,2,3:T(8,128)S(1)} reshape(f32[16,8,16,8]{3,2,1,0:T(8,128)} %get-tuple-element.24) | data formatting | bytes 131072 | tf_op jit(solution)/shard_map/jit(kron)/mul | solution.py:56
  10.2 0.1 broadcast_in_dim.177
  10.4 0.1 broadcast_in_dim.173
  10.9 1.7 %reshape.406 = f32[128,128,1,1]{1,0,2,3:T(8,128)S(1)} reshape(f32[16,8,16,8]{3,2,1,0:T(8,128)} %get-tuple-element.23) | data formatting | bytes 131072 | tf_op jit(solution)/shard_map/jit(kron)/mul | solution.py:56
  12.6 0.3 copy.189
  12.9 2.4 %convolution_bitcast_fusion.3 = f32[8,8,16,128]{3,2,1,0:T(8,128)} fusion(f32[8,8,16,128]{3,0,2,1:T(8,128)} %get-tuple-element.32, f32[128,128,1,1]{1,0,2,3:T(8,128)S(1)} %reshape.403), kind=kOutput, calls=%fused_computation.40 | convolution fusion | flops 201326592 | bytes 1114112 | tf_op jit(solution)/shard_map/xynb,ab->xyna/dot_general | solution.py:63
  15.3 0.6 convolution_bitcast_fusion.5
  16.2 0.1 broadcast_in_dim.161
  16.3 1.6 %convolution_bitcast_fusion.4 = f32[8,8,16,128]{3,2,1,0:T(8,128)S(1)} fusion(f32[8,8,16,128]{3,0,2,1:T(8,128)} %get-tuple-element.33, f32[128,128,1,1]{1,0,2,3:T(8,128)S(1)} %reshape.403), kind=kOutput, calls=%fused_computation.41 | convolution fusion | flops 201326592 | bytes 1114112 | tf_op jit(solution)/shard_map/xynb,ab->xyna/dot_general | solution.py:63
  18.0 3.2 %convolution_bitcast_fusion = f32[8,8,2048]{2,0,1:T(8,128)} fusion(f32[8,8,2048]{2,0,1:T(8,128)S(1)} %fusion.32, f32[8,8,16,128]{3,2,1,0:T(8,128)} %convolution_bitcast_fusion.3, f32[8,8,2048]{2,0,1:T(8,128)S(1)} %fusion.18, f32[2048]{0:T(1024)S(1)} %broadcast_in_dim.177, f32[2048]{0:T(1024)S(1)} %broadcast_in_dim.173, f32[2048]{0:T(1024)S(1)} %broadcast_in_dim.165, ...), kind=kOutput, calls=%fused_computation.18 | convolution fusion | flops 202244096 | bytes 2195712 | tf_op jit(solution)/shard_map/xynb,ab->xyna/dot_general | solution.py:63
  21.2 2.0 %convolution_bitcast_fusion.1 = f32[8,8,2048]{2,0,1:T(8,128)} fusion(f32[8,8,2048]{2,0,1:T(8,128)S(1)} %fusion.42, f32[8,8,16,128]{3,2,1,0:T(8,128)S(1)} %convolution_bitcast_fusion.4, f32[8,8,2048]{2,0,1:T(8,128)S(1)} %fusion.20, f32[2048]{0:T(1024)S(1)} %broadcast_in_dim.177, f32[2048]{0:T(1024)S(1)} %broadcast_in_dim.173, ...), kind=kOutput, calls=%fused_computation.19 | convolution fusion | flops 202244096 | bytes 2195712 | tf_op jit(solution)/shard_map/xynb,ab->xyna/dot_general | solution.py:63
  23.2 4.0 %multiply_multiply_fusion.7 = (f32[8,8,2048]{2,0,1:T(8,128)}, f32[8,8,2048]{2,0,1:T(8,128)}, f32[8,8,2048]{2,0,1:T(8,128)S(1)}, f32[8,8,2048]{2,0,1:T(8,128)}) fusion(f32[8,8,16,128]{3,2,1,0:T(8,128)S(1)} %convolution_bitcast_fusion.5, f32[8,8,2048]{2,0,1:T(8,128)S(1)} %fusion.22, f32[2048]{0:T(1024)S(1)} %broadcast_in_dim.173, ...), kind=kOutput, calls=%fused_computation.7 | convolution fusion | flops 15073280 | bytes 6849024 | tf_op jit(solution)/shard_map/nbyz,ab->nayz/dot_general | solution.py:63
  27.2 1.6 %fusion.54 = f32[8,8,2048]{2,0,1:T(8,128)} fusion(f32[8,8,1]{1,0,2:T(8,128)S(1)} %copy-done.12, f32[8,8,2048]{2,0,1:T(8,128)S(1)} %get-tuple-element.22), kind=kOutput, calls=%fused_computation.94 | convolution fusion | flops 12582912 | bytes 1048832 | tf_op jit(solution)/shard_map/xnbz,ab->xnaz/dot_general | solution.py:63
  29.0 1.9 %fusion.57 = f32[8,8,2048]{2,0,1:T(8,128)S(1)} fusion(f32[8,8,1]{1,0,2:T(8,128)S(1)} %copy-done.12, f32[8,8,2048]{2,0,1:T(8,128)} %get-tuple-element.21), kind=kOutput, calls=%fused_computation.97 | convolution fusion | flops 12582912 | bytes 1048832 | tf_op jit(solution)/shard_map/xnbz,ab->xnaz/dot_general | solution.py:63
  31.0 2.3 %convolution_bitcast_fusion.2 = f32[8,8,2048]{2,0,1:T(8,128)S(1)} fusion(f32[8,8,2048]{2,0,1:T(8,128)} %get-tuple-element.31, f32[8,8,16,128]{3,2,1,0:T(8,128)S(1)} %convolution_bitcast_fusion.5, f32[8,8,2048]{2,0,1:T(8,128)S(1)} %fusion.22, f32[2048]{0:T(1024)S(1)} %broadcast_in_dim.177, f32[2048]{0:T(1024)S(1)} %broadcast_in_dim.173, ...), kind=kOutput, calls=%fused_computation.20 | convolution fusion | flops 202244096 | bytes 2195712 | tf_op jit(solution)/shard_map/xynb,ab->xyna/dot_general | solution.py:63
  33.3 0.8 %fusion.60 = f32[8,8,2048]{2,0,1:T(8,128)S(1)} fusion(f32[8,8,1]{1,0,2:T(8,128)S(1)} %copy-done.12, f32[8,8,2048]{2,0,1:T(8,128)S(1)} %copy-done.11), kind=kOutput, calls=%fused_computation.100 | convolution fusion | flops 12582912 | bytes 1048832 | tf_op jit(solution)/shard_map/xnbz,ab->xnaz/dot_general | solution.py:63
  34.2 1.5 %fusion.5 = f32[1,8,8,2048]{3,1,2,0:T(8,128)S(1)} fusion(f32[8,8,2048]{2,0,1:T(8,128)S(1)} %copy-done.10, f32[8,8,1]{1,0,2:T(8,128)S(1)} %copy-done.12, f32[8,8,2048]{2,0,1:T(8,128)S(1)} %copy-done.8, f32[8,8,2048]{2,0,1:T(8,128)S(1)} %fusion.32, f32[8,8,16,128]{3,2,1,0:T(8,128)S(1)} %copy-done.1, f32[8,8,2048]{2,0,1:T(8,128)S(1)} %fusion.18, ...), kind=kOutput, calls=%fused_computation.17 | convolution fusion | flops 13762560 | bytes 3179008 | tf_op jit(solution)/shard_map/nbyz,ab->nayz/dot_general | solution.py:63
  35.7 1.4 %fusion.4 = f32[1,8,8,2048]{3,1,2,0:T(8,128)S(1)} fusion(f32[8,8,2048]{2,0,1:T(8,128)S(1)} %copy-done.9, f32[8,8,1]{1,0,2:T(8,128)S(1)} %copy-done.12, f32[8,8,2048]{2,0,1:T(8,128)S(1)} %fusion.57, f32[8,8,2048]{2,0,1:T(8,128)S(1)} %fusion.42, f32[8,8,16,128]{3,2,1,0:T(8,128)S(1)} %copy-done.3, f32[8,8,2048]{2,0,1:T(8,128)S(1)} %fusion.20, ...), kind=kOutput, calls=%fused_computation.16 | convolution fusion | flops 13762560 | bytes 3179008 | tf_op jit(solution)/shard_map/nbyz,ab->nayz/dot_general | solution.py:63
  37.2 1.4 %fusion.3 = f32[1,8,8,2048]{3,1,2,0:T(8,128)S(1)} fusion(f32[8,8,2048]{2,0,1:T(8,128)S(1)} %convolution_bitcast_fusion.2, f32[8,8,1]{1,0,2:T(8,128)S(1)} %copy-done.12, f32[8,8,2048]{2,0,1:T(8,128)S(1)} %fusion.60, f32[8,8,2048]{2,0,1:T(8,128)S(1)} %copy-done.5, f32[8,8,16,128]{3,2,1,0:T(8,128)S(1)} %convolution_bitcast_fusion.5, ...), kind=kOutput, calls=%fused_computation.15 | convolution fusion | flops 13762560 | bytes 3179008 | tf_op jit(solution)/shard_map/nbyz,ab->nayz/dot_general | solution.py:63
  38.6 0.1 pad_maximum_fusion
  38.8 0.3 fusion.132
  39.0 4.1 %collective-permute-start = (f32[3,1,8,2048]{3,1,2,0:T(1,128)S(1)}, f32[3,1,8,2048]{3,1,2,0:T(1,128)S(1)}, u32[]{:S(2)}, u32[]{:S(2)}) collective-permute-start(f32[3,1,8,2048]{3,1,2,0:T(1,128)S(1)} %get-tuple-element.14), channel_id=1, source_target_pairs={{128,0},{256,128},{384,256},{129,1},{257,129},{385,257},{130,2},{2... | collective-permute-start | bytes 589832 | tf_op jit(solution)/shard_map/ppermute | solution.py:22
  43.1 1.3 %collective-permute-start.1 = (f32[3,1,8,2048]{3,1,2,0:T(1,128)S(1)}, f32[3,1,8,2048]{3,1,2,0:T(1,128)S(1)}, u32[]{:S(2)}, u32[]{:S(2)}) collective-permute-start(f32[3,1,8,2048]{3,1,2,0:T(1,128)S(1)} %get-tuple-element.13), channel_id=1, source_target_pairs={{0,128},{128,256},{256,384},{1,129},{129,257},{257,385},{2,130},{1... | collective-permute-start | bytes 589832 | tf_op jit(solution)/shard_map/ppermute | solution.py:22
  44.4 0.4 fusion.133
  44.8 2.5 %collective-permute-done = f32[3,1,8,2048]{3,1,2,0:T(1,128)S(1)} collective-permute-done((f32[3,1,8,2048]{3,1,2,0:T(1,128)S(1)}, f32[3,1,8,2048]{3,1,2,0:T(1,128)S(1)}, u32[]{:S(2)}, u32[]{:S(2)}) %collective-permute-start) | collective-permute-done | bytes 196640 | tf_op jit(solution)/shard_map/ppermute | solution.py:22
  47.3 8.9 %collective-permute-done.1 = f32[3,1,8,2048]{3,1,2,0:T(1,128)S(1)} collective-permute-done((f32[3,1,8,2048]{3,1,2,0:T(1,128)S(1)}, f32[3,1,8,2048]{3,1,2,0:T(1,128)S(1)}, u32[]{:S(2)}, u32[]{:S(2)}) %collective-permute-start.1) | collective-permute-done | bytes 196640 | tf_op jit(solution)/shard_map/ppermute | solution.py:22
  56.2 0.8 fusion.7
  57.1 3.6 %collective-permute-start.2 = (f32[3,8,1,2048]{3,1,2,0:T(8,128)S(1)}, f32[3,8,1,2048]{3,1,2,0:T(8,128)S(1)}, u32[]{:S(2)}, u32[]{:S(2)}) collective-permute-start(f32[3,8,1,2048]{3,1,2,0:T(8,128)S(1)} %get-tuple-element.10), channel_id=1, source_target_pairs={{8,0},{16,8},{24,16},{32,24},{40,32},{48,40},{56,48},{64,56},{72,6... | collective-permute-start | bytes 589832 | tf_op jit(solution)/shard_map/ppermute | solution.py:22
  60.6 3.2 %collective-permute-start.3 = (f32[3,8,1,2048]{3,1,2,0:T(8,128)S(1)}, f32[3,8,1,2048]{3,1,2,0:T(8,128)S(1)}, u32[]{:S(2)}, u32[]{:S(2)}) collective-permute-start(f32[3,8,1,2048]{3,1,2,0:T(8,128)S(1)} %get-tuple-element.9), channel_id=1, source_target_pairs={{0,8},{8,16},{16,24},{24,32},{32,40},{40,48},{48,56},{56,64},{64,7... | collective-permute-start | bytes 589832 | tf_op jit(solution)/shard_map/ppermute | solution.py:22
  63.8 0.3 fusion.131
  64.1 3.5 %collective-permute-done.2 = f32[3,8,1,2048]{3,1,2,0:T(8,128)S(1)} collective-permute-done((f32[3,8,1,2048]{3,1,2,0:T(8,128)S(1)}, f32[3,8,1,2048]{3,1,2,0:T(8,128)S(1)}, u32[]{:S(2)}, u32[]{:S(2)}) %collective-permute-start.2) | collective-permute-done | bytes 196640 | tf_op jit(solution)/shard_map/ppermute | solution.py:22
  67.6 1.6 %collective-permute-done.3 = f32[3,8,1,2048]{3,1,2,0:T(8,128)S(1)} collective-permute-done((f32[3,8,1,2048]{3,1,2,0:T(8,128)S(1)}, f32[3,8,1,2048]{3,1,2,0:T(8,128)S(1)}, u32[]{:S(2)}, u32[]{:S(2)}) %collective-permute-start.3) | collective-permute-done | bytes 196640 | tf_op jit(solution)/shard_map/ppermute | solution.py:22
  69.2 0.5 fusion.9
  69.8 1.9 %collective-permute-start.4 = (f32[3,8,8,1]{3,1,2,0:T(8,128)S(1)}, f32[3,8,8,1]{3,1,2,0:T(8,128)S(1)}, u32[]{:S(2)}, u32[]{:S(2)}) collective-permute-start(f32[3,8,8,1]{3,1,2,0:T(8,128)S(1)} %get-tuple-element.6), channel_id=1, source_target_pairs={{1,0},{2,1},{3,2},{4,3},{5,4},{6,5},{7,6},{9,8},{10,9},{11,10},{12... | collective-permute-start | bytes 2312 | tf_op jit(solution)/shard_map/ppermute | solution.py:22
  71.7 2.4 %collective-permute-start.5 = (f32[3,8,8,1]{3,1,2,0:T(8,128)S(1)}, f32[3,8,8,1]{3,1,2,0:T(8,128)S(1)}, u32[]{:S(2)}, u32[]{:S(2)}) collective-permute-start(f32[3,8,8,1]{3,1,2,0:T(8,128)S(1)} %get-tuple-element.5), channel_id=1, source_target_pairs={{0,1},{1,2},{2,3},{3,4},{4,5},{5,6},{6,7},{8,9},{9,10},{10,11},{11... | collective-permute-start | bytes 2312 | tf_op jit(solution)/shard_map/ppermute | solution.py:22
  74.1 0.6 fusion.129
  74.7 2.9 %collective-permute-done.5 = f32[3,8,8,1]{3,1,2,0:T(8,128)S(1)} collective-permute-done((f32[3,8,8,1]{3,1,2,0:T(8,128)S(1)}, f32[3,8,8,1]{3,1,2,0:T(8,128)S(1)}, u32[]{:S(2)}, u32[]{:S(2)}) %collective-permute-start.5) | collective-permute-done | bytes 800 | tf_op jit(solution)/shard_map/ppermute | solution.py:22
  77.7 0.7 fusion.11
  78.4 2.1 %copy.76 = f32[3,8,8,2048]{3,2,1,0:T(8,128)} copy(f32[3,8,8,2048]{3,1,2,0:T(8,128)S(1)} %fusion.11) | data formatting | bytes 3145728 | tf_op jit(solution)/shard_map/add | solution.py:111
  (54 shorter events, 1.3 us)
Async XLA Ops:
  0.0 1.9 %copy-start.4 = (f32[3,8,8,2048]{3,2,1,0:T(8,128)S(1)}, f32[3,8,8,2048]{3,2,1,0:T(8,128)}, u32[]{:S(2)}) copy-start(f32[3,8,8,2048]{3,2,1,0:T(8,128)} %param.8) | copy-start | bytes 4718596
  0.0 1.9 %copy-start.12 = (f32[8,8,1]{1,0,2:T(8,128)S(1)}, f32[8,8,1]{1,0,2:T(8,128)}, u32[]{:S(2)}) copy-start(f32[8,8,1]{1,0,2:T(8,128)} %constant.40) | copy-start | bytes 772
  1.9 10.7 %copy-start.6 = (f32[1,8,8,2048]{3,2,1,0:T(8,128)}, f32[1,8,8,2048]{3,2,1,0:T(8,128)S(1)}, u32[]{:S(2)}) copy-start(f32[1,8,8,2048]{3,2,1,0:T(8,128)S(1)} %get-tuple-element.17) | copy-start | bytes 1572868
  4.4 2.5 %copy-start.15 = (f32[8,8]{1,0:T(8,128)S(1)}, f32[8,8]{1,0:T(8,128)}, u32[]{:S(2)}) copy-start(f32[8,8]{1,0:T(8,128)} %constant.39) | copy-start | bytes 772
  4.4 2.4 %copy-start.16 = (f32[8,8]{1,0:T(8,128)S(1)}, f32[8,8]{1,0:T(8,128)}, u32[]{:S(2)}) copy-start(f32[8,8]{1,0:T(8,128)} %constant.35.clone) | copy-start | bytes 772
  6.9 3.2 %copy-start.13 = (f32[6,1,1,256]{3,2,1,0:T(1,128)S(1)}, f32[6,1,1,256]{3,2,1,0:T(1,128)}, u32[]{:S(2)}) copy-start(f32[6,1,1,256]{3,2,1,0:T(1,128)} %param.9) | copy-start | bytes 18436
  6.9 3.8 %copy-start.14 = (f32[8]{0:T(128)S(1)}, f32[8]{0:T(128)}, u32[]{:S(2)}) copy-start(f32[8]{0:T(128)} %constant.36.clone) | copy-start | bytes 100
  18.0 5.2 %copy-start.2 = (f32[8,8,16,128]{3,2,1,0:T(8,128)}, f32[8,8,16,128]{3,2,1,0:T(8,128)S(1)}, u32[]{:S(2)}) copy-start(f32[8,8,16,128]{3,2,1,0:T(8,128)S(1)} %convolution_bitcast_fusion.4) | copy-start | bytes 1572868
  21.2 2.0 %copy-start = (f32[8,8,16,128]{3,2,1,0:T(8,128)S(1)}, f32[8,8,16,128]{3,2,1,0:T(8,128)}, u32[]{:S(2)}) copy-start(f32[8,8,16,128]{3,2,1,0:T(8,128)} %convolution_bitcast_fusion.3) | copy-start | bytes 1572868
  21.2 2.0 %copy-start.7 = (f32[1,8,8,2048]{3,2,1,0:T(8,128)S(1)}, f32[1,8,8,2048]{3,2,1,0:T(8,128)}, u32[]{:S(2)}) copy-start(f32[1,8,8,2048]{3,2,1,0:T(8,128)} %copy-done.6) | copy-start | bytes 1572868
  29.0 4.3 %copy-start.11 = (f32[8,8,2048]{2,0,1:T(8,128)S(1)}, f32[8,8,2048]{2,0,1:T(8,128)}, u32[]{:S(2)}) copy-start(f32[8,8,2048]{2,0,1:T(8,128)} %get-tuple-element.20) | copy-start | bytes 1572868
  30.9 3.2 %copy-start.1 = (f32[8,8,16,128]{3,2,1,0:T(8,128)S(1)}, f32[8,8,16,128]{3,2,1,0:T(8,128)}, u32[]{:S(2)}) copy-start(f32[8,8,16,128]{3,2,1,0:T(8,128)} %convolution_bitcast_fusion.3) | copy-start | bytes 1572868
  31.0 3.2 %copy-start.8 = (f32[8,8,2048]{2,0,1:T(8,128)S(1)}, f32[8,8,2048]{2,0,1:T(8,128)}, u32[]{:S(2)}) copy-start(f32[8,8,2048]{2,0,1:T(8,128)} %fusion.54) | copy-start | bytes 1572868
  31.0 3.2 %copy-start.10 = (f32[8,8,2048]{2,0,1:T(8,128)S(1)}, f32[8,8,2048]{2,0,1:T(8,128)}, u32[]{:S(2)}) copy-start(f32[8,8,2048]{2,0,1:T(8,128)} %convolution_bitcast_fusion) | copy-start | bytes 1572868
  34.2 1.5 %copy-start.3 = (f32[8,8,16,128]{3,2,1,0:T(8,128)S(1)}, f32[8,8,16,128]{3,2,1,0:T(8,128)}, u32[]{:S(2)}) copy-start(f32[8,8,16,128]{3,2,1,0:T(8,128)} %copy-done.2) | copy-start | bytes 1572868
  34.2 1.5 %copy-start.9 = (f32[8,8,2048]{2,0,1:T(8,128)S(1)}, f32[8,8,2048]{2,0,1:T(8,128)}, u32[]{:S(2)}) copy-start(f32[8,8,2048]{2,0,1:T(8,128)} %convolution_bitcast_fusion.1) | copy-start | bytes 1572868
  35.7 1.5 %copy-start.5 = (f32[8,8,2048]{2,0,1:T(8,128)S(1)}, f32[8,8,2048]{2,0,1:T(8,128)}, u32[]{:S(2)}) copy-start(f32[8,8,2048]{2,0,1:T(8,128)} %get-tuple-element.31) | copy-start | bytes 1572868
  39.0 8.2 %collective-permute-start = (f32[3,1,8,2048]{3,1,2,0:T(1,128)S(1)}, f32[3,1,8,2048]{3,1,2,0:T(1,128)S(1)}, u32[]{:S(2)}, u32[]{:S(2)}) collective-permute-start(f32[3,1,8,2048]{3,1,2,0:T(1,128)S(1)} %get-tuple-element.14), channel_id=1, source_target_pairs={{128,0},{256,128},{384,256},{129,1},{257,129},{385,257},{130,2},{2... | collective-permute-start | bytes 589832 | tf_op jit(solution)/shard_map/ppermute | solution.py:22
  43.1 13.1 %collective-permute-start.1 = (f32[3,1,8,2048]{3,1,2,0:T(1,128)S(1)}, f32[3,1,8,2048]{3,1,2,0:T(1,128)S(1)}, u32[]{:S(2)}, u32[]{:S(2)}) collective-permute-start(f32[3,1,8,2048]{3,1,2,0:T(1,128)S(1)} %get-tuple-element.13), channel_id=1, source_target_pairs={{0,128},{128,256},{256,384},{1,129},{129,257},{257,385},{2,130},{1... | collective-permute-start | bytes 589832 | tf_op jit(solution)/shard_map/ppermute | solution.py:22
  57.1 10.6 %collective-permute-start.2 = (f32[3,8,1,2048]{3,1,2,0:T(8,128)S(1)}, f32[3,8,1,2048]{3,1,2,0:T(8,128)S(1)}, u32[]{:S(2)}, u32[]{:S(2)}) collective-permute-start(f32[3,8,1,2048]{3,1,2,0:T(8,128)S(1)} %get-tuple-element.10), channel_id=1, source_target_pairs={{8,0},{16,8},{24,16},{32,24},{40,32},{48,40},{56,48},{64,56},{72,6... | collective-permute-start | bytes 589832 | tf_op jit(solution)/shard_map/ppermute | solution.py:22
  60.6 8.6 %collective-permute-start.3 = (f32[3,8,1,2048]{3,1,2,0:T(8,128)S(1)}, f32[3,8,1,2048]{3,1,2,0:T(8,128)S(1)}, u32[]{:S(2)}, u32[]{:S(2)}) collective-permute-start(f32[3,8,1,2048]{3,1,2,0:T(8,128)S(1)} %get-tuple-element.9), channel_id=1, source_target_pairs={{0,8},{8,16},{16,24},{24,32},{32,40},{40,48},{48,56},{56,64},{64,7... | collective-permute-start | bytes 589832 | tf_op jit(solution)/shard_map/ppermute | solution.py:22
  69.8 4.9 %collective-permute-start.4 = (f32[3,8,8,1]{3,1,2,0:T(8,128)S(1)}, f32[3,8,8,1]{3,1,2,0:T(8,128)S(1)}, u32[]{:S(2)}, u32[]{:S(2)}) collective-permute-start(f32[3,8,8,1]{3,1,2,0:T(8,128)S(1)} %get-tuple-element.6), channel_id=1, source_target_pairs={{1,0},{2,1},{3,2},{4,3},{5,4},{6,5},{7,6},{9,8},{10,9},{11,10},{12... | collective-permute-start | bytes 2312 | tf_op jit(solution)/shard_map/ppermute | solution.py:22
  71.7 5.9 %collective-permute-start.5 = (f32[3,8,8,1]{3,1,2,0:T(8,128)S(1)}, f32[3,8,8,1]{3,1,2,0:T(8,128)S(1)}, u32[]{:S(2)}, u32[]{:S(2)}) collective-permute-start(f32[3,8,8,1]{3,1,2,0:T(8,128)S(1)} %get-tuple-element.5), channel_id=1, source_target_pairs={{0,1},{1,2},{2,3},{3,4},{4,5},{5,6},{6,7},{8,9},{9,10},{10,11},{11... | collective-permute-start | bytes 2312 | tf_op jit(solution)/shard_map/ppermute | solution.py:22
where the time goes:
time: 80.9 us; the launch traced here: 80.4 us
  matrix products  28.1 us (35%)
  waiting for transfers between devices  19.4 us (24%)
  starting transfers between devices  16.4 us (20%)
  local copies, waits for them, and re-layouts  12.2 us (15%)
  other arithmetic  3.76 us (5%)
    dot_general x18, matrix products, apply_axis(): jnp.einsum(patterns[direction], folded_field, big_table, precision=lax.Pr...  28.1 us
    ppermute x6, waiting for transfers between devices, shifted(): return lax.ppermute(array, axis, pairs)  19.4 us
    ppermute x6, starting transfers between devices, shifted(): return lax.ppermute(array, axis, pairs)  16.4 us
    mul x2, local copies, waits for them, and re-layouts, apply_axis(): big_table = jnp.kron(jnp.eye(block_size // 8, dtype=jnp.float32), matrix)  3.3 us
    add x1, local copies, waits for them, and re-layouts, combine(): middle + jnp.where(position == 7, from_above, 0.0)  2.06 us
    add x3, other arithmetic, combine(): middle + jnp.where(position == 7, from_above, 0.0)  2 us
  transfers between devices with their start and end apart: 6, of which 5 were waited for; matrix products, arithmetic and copies ran while one was open for 2% of the time, Pallas kernels for 0%

commit v1 on v0

v1 whole, which is shorter than its diff:
```python
import functools

import jax
import jax.numpy as jnp
import numpy as np
from jax import lax
from jax.experimental import pallas as pl
from jax.experimental.pallas import tpu as pltpu
from jax.sharding import PartitionSpec as P

MESH = pl.DeviceIdType.MESH
F32 = jnp.float32
BF16 = jnp.bfloat16
LANES = 128

interior_points = [
    -0.8717401485096066,
    -0.5917001814331423,
    -0.2092992179024789,
    0.2092992179024789,
    0.5917001814331423,
    0.8717401485096066,
]


def legendre_seven(point):
    previous = 1.0
    current = point
    for order in range(1, 7):
        following = ((2 * order + 1) * point * current - order * previous) / (order + 1)
        previous = current
        current = following
    return current


def gll_tables():
    degree = 7
    points = [-1.0] + interior_points + [1.0]
    values = [legendre_seven(point) for point in points]
    node_count = degree + 1
    weights = np.array([2.0 / (degree * (degree + 1) * value * value) for value in values])
    derivative = np.zeros((node_count, node_count))
    for row_index in range(node_count):
        for col_index in range(node_count):
            if row_index != col_index:
                derivative[row_index, col_index] = values[row_index] / (
                    values[col_index] * (points[row_index] - points[col_index])
                )
    derivative[0, 0] = -degree * (degree + 1) / 4.0
    derivative[node_count - 1, node_count - 1] = degree * (degree + 1) / 4.0
    return derivative, weights


DERIVATIVE, WEIGHTS = gll_tables()
WEIGHTS = [float(w) for w in WEIGHTS]


def halves(matrix):
    plus = [[float(0.5 * (matrix[a, b] - matrix[a, 7 - b])) for b in range(4)] for a in range(4)]
    minus = [[float(0.5 * (matrix[a, b] + matrix[a, 7 - b])) for b in range(4)] for a in range(4)]
    return plus, minus


GRAD = halves(DERIVATIVE)
BACK = halves(DERIVATIVE.T)
BACK_X = halves(DERIVATIVE.T * np.array(WEIGHTS)[None, :])


def apply_halves(tables, planes):
    plus, minus = tables
    diff = [planes[b] - planes[7 - b] for b in range(4)]
    total = [planes[b] + planes[7 - b] for b in range(4)]
    out = [None] * 8
    for a in range(4):
        p = plus[a][0] * diff[0]
        q = minus[a][0] * total[0]
        for b in range(1, 4):
            p = p + plus[a][b] * diff[b]
            q = q + minus[a][b] * total[b]
        out[a] = p + q
        out[7 - a] = p - q
    return out


def lane_table(matrix):
    full = np.kron(np.eye(16), matrix).astype(np.float32)
    high = full.astype(BF16).astype(np.float32)
    row = np.concatenate([high, full - high], axis=1)
    return np.concatenate([row, row], axis=0).astype(BF16)


def lane_apply(rows, table):
    high = rows.astype(BF16)
    low = (rows - high.astype(F32)).astype(BF16)
    both = jnp.dot(jnp.concatenate([high, low], axis=1), table, preferred_element_type=F32)
    return both[:, :LANES] + both[:, LANES:]


def weight_vector(index):
    out = jnp.full(index.shape, WEIGHTS[0], F32)
    for i in range(1, 8):
        out = jnp.where(index % 8 == i, WEIGHTS[i], out)
    return out


def exchange_kernel(
    sizes,
    u_hbm, g_ref, tables_hbm, o_ref,
    u_t, l_t, tab, geo, s_gy, s_gz, s_fy, s_fz,
    xf, yf, rx, ry, zr, edge, edge_y, edge_x, send_y, send_x,
    in_sem, tab_sem, xs, xr, ys, yr, zs, zrs, eys, eyr, exs, exr,
):
    nx, ny, nz = sizes
    ix, iy, iz = lax.axis_index("gx"), lax.axis_index("gy"), lax.axis_index("gz")
    parity = iy % 2
    has_x = [ix > 0, ix < nx - 1]
    has_y = [iy > 0, iy < ny - 1]
    has_z = [iz > 0, iz < nz - 1]
    no_x = [ix == 0, ix == nx - 1]
    no_y = [iy == 0, iy == ny - 1]
    step_of = [-1, 1]

    def load(t):
        return pltpu.make_async_copy(
            u_hbm.at[:, pl.ds(pl.multiple_of(t * LANES, LANES), LANES)], u_t.at[t], in_sem.at[t]
        )

    tile_order = [4, 5, 6, 7, 0, 15, 8, 9, 10, 11, 1, 2, 3, 12, 13, 14]
    table_copy = pltpu.make_async_copy(tables_hbm, tab, tab_sem)
    load(tile_order[0]).start()
    table_copy.start()
    for t in tile_order[1:]:
        load(t).start()

    barrier = pltpu.get_barrier_semaphore()
    dxm = 2 * parity - 1
    mid_x = [(parity == s) & has_x[s] for s in range(2)]
    greet = []
    for s in range(2):
        greet.append((has_x[s], {"gx": ix + step_of[s]}))
        greet.append((has_y[s], {"gy": iy + step_of[s]}))
        greet.append((has_z[s], {"gz": iz + step_of[s]}))
        for r in range(2):
            greet.append((mid_x[s] & has_y[r], {"gx": ix + step_of[s], "gy": iy + step_of[r]}))
    for there, device in greet:

        @pl.when(there)
        def _(device=device):
            pl.semaphore_signal(barrier, inc=1, device_id=device, device_id_type=MESH)

    sub = lax.broadcasted_iota(jnp.int32, (8, LANES), 0)
    lane = lax.broadcasted_iota(jnp.int32, (8, LANES), 1)
    plane_weight = weight_vector(sub) * weight_vector(lane)
    for half in range(2):
        for k in range(6):
            row = jnp.broadcast_to(g_ref[k, 0, :, half * LANES:(half + 1) * LANES], (8, LANES))
            for j in range(8):
                picked = jnp.take_along_axis(row, lane // 8 + 16 * j, axis=1)
                geo[half * 8 + j, 8 * k:8 * k + 8, :] = picked * plane_weight

    for s in range(2):

        @pl.when(no_x[s])
        def _(s=s):
            rx[s] = jnp.zeros(rx.shape[1:], F32)

        @pl.when(no_y[s])
        def _(s=s):
            ry[s] = jnp.zeros(ry.shape[1:], F32)

        for r in range(2):
            corner = 2 * s + r

            @pl.when(no_y[r])
            def _(corner=corner):
                edge_y[corner] = jnp.zeros(edge_y.shape[1:], F32)

            @pl.when(no_x[s] | ((parity != s) & has_y[r]))
            def _(corner=corner):
                edge_x[corner] = jnp.zeros(edge_x.shape[1:], F32)

    def compute(t):
        s_gz[...] = lane_apply(u_t[t], tab[0])
        for c in range(3):
            base = 64 * c
            uy = [u_t[t, pl.ds(base + y, 8, stride=8), :] for y in range(8)]
            gy = apply_halves(GRAD, uy)
            for y in range(8):
                s_gy[pl.ds(base + y, 8, stride=8), :] = gy[y]
        g00, g11, g22, g01, g02, g12 = [geo[t, 8 * k:8 * k + 8, :] for k in range(6)]
        for c in range(3):
            base = 64 * c
            ux = [u_t[t, base + 8 * x:base + 8 * x + 8, :] for x in range(8)]
            gx = apply_halves(GRAD, ux)
            fx = []
            for x in range(8):
                rows = slice(base + 8 * x, base + 8 * x + 8)
                a, b, d = gx[x], s_gy[rows, :], s_gz[rows, :]
                fx.append(g00 * a + g01 * b + g02 * d)
                s_fy[rows, :] = g01 * a + g11 * b + g12 * d
                s_fz[rows, :] = g02 * a + g12 * b + g22 * d
            ox = apply_halves(BACK_X, fx)
            for x in range(8):
                l_t[t, base + 8 * x:base + 8 * x + 8, :] = ox[x]
        s_gz[...] = lane_apply(s_fz[...], tab[1])
        for c in range(3):
            base = 64 * c
            fy = [s_fy[pl.ds(base + y, 8, stride=8), :] for y in range(8)]
            oy = apply_halves(BACK, fy)
            for y in range(8):
                s_gy[pl.ds(base + y, 8, stride=8), :] = oy[y]
        for c in range(3):
            base = 64 * c
            for x in range(8):
                rows = slice(base + 8 * x, base + 8 * x + 8)
                l_t[t, rows, :] = l_t[t, rows, :] + WEIGHTS[x] * (s_gy[rows, :] + s_gz[rows, :])

    def faces(t):
        ch, tt = t // 4, t % 4
        for c in range(3):
            at = pl.ds(4 + 4 * c + tt, 8, stride=12)
            for s in range(2):
                first = 64 * c + 56 * s
                xf[s, ch, at, :] = l_t[t, first:first + 8, :]
                yf[s, ch, at, :] = l_t[t, pl.ds(64 * c + 7 * s, 8, stride=8), :]

    body = pl.ds(16, 72)

    def face_copy(buf, land, send, recv, axis, index, s, ch):
        return pltpu.make_async_remote_copy(
            src_ref=buf.at[s, ch, body], dst_ref=land.at[1 - s, ch, body],
            send_sem=send.at[s, ch], recv_sem=recv.at[1 - s, ch],
            device_id={axis: index + step_of[s]}, device_id_type=MESH,
        )

    def x_copy(s, ch):
        return face_copy(xf, rx, xs, xr, "gx", ix, s, ch)

    def y_copy(s, ch):
        return face_copy(yf, ry, ys, yr, "gy", iy, s, ch)

    def send_faces(ch):
        for s in range(2):

            @pl.when(has_x[s])
            def _(s=s):
                x_copy(s, ch).start()

            @pl.when(has_y[s])
            def _(s=s):
                y_copy(s, ch).start()

    def z_copy(s):
        return pltpu.make_async_remote_copy(
            src_ref=l_t.at[15 * s], dst_ref=zr.at[1 - s], send_sem=zs.at[s], recv_sem=zrs.at[1 - s],
            device_id={"gz": iz + step_of[s]}, device_id_type=MESH,
        )

    table_copy.wait()

    def step(i, carry):
        t = jnp.where(
            i < 4, i + 4,
            jnp.where(i < 6, (i - 4) * 15, jnp.where(i < 10, i + 2, jnp.where(i < 13, i - 9, i - 1))),
        )
        load(t).wait()
        compute(t)
        faces(t)

        @pl.when(i == 3)
        def _():
            pl.semaphore_wait(barrier, sum(there.astype(jnp.int32) for there, _ in greet))
            send_faces(1)

        @pl.when(i == 5)
        def _():
            for s in range(2):

                @pl.when(has_z[s])
                def _(s=s):
                    z_copy(s).start()

        return carry

    lax.fori_loop(0, 16, step, 0)

    wide = lax.broadcasted_iota(jnp.int32, (192, LANES), 1)
    for s in range(2):

        @pl.when(has_z[s])
        def _(s=s):
            z_copy(s).wait_send()
            z_copy(1 - s).wait_recv()
            landed = pltpu.roll(zr[s], 1 if s == 0 else LANES - 1, 1)
            l_t[15 * s] = l_t[15 * s] + jnp.where(wide == (LANES - 1) * s, landed, 0.0)
            faces(15 * s)

    for s in range(2):
        for r in range(2):
            for ch in range(4):
                first = 4 + 84 * r
                edge[2 * s + r, 12 * ch:12 * ch + 12, :] = xf[s, ch, first:first + 12, :]

    def along_y(s, r, buf):
        k, there = 2 * s + r, 2 * s + 1 - r
        return pltpu.make_async_remote_copy(
            src_ref=buf.at[k], dst_ref=edge_y.at[there], send_sem=eys.at[k], recv_sem=eyr.at[there],
            device_id={"gy": iy + step_of[r]}, device_id_type=MESH,
        )

    def along_x(s, r, buf, diagonal):
        k, there = 2 * s + r, 2 * (1 - s) + (1 - r if diagonal else r)
        device = {"gx": ix + step_of[s]}
        if diagonal:
            device["gy"] = iy + step_of[r]
        return pltpu.make_async_remote_copy(
            src_ref=buf.at[k], dst_ref=edge_x.at[there], send_sem=exs.at[k], recv_sem=exr.at[there],
            device_id=device, device_id_type=MESH,
        )

    corners = [(s, r) for s in range(2) for r in range(2)]
    middle = {(s, r): mid_x[s] & has_y[r] for s, r in corners}
    ends = {(s, r): has_y[r] & ((parity != s) | no_x[s]) for s, r in corners}
    alone = {(s, r): has_x[s] & no_y[r] for s, r in corners}

    for s, r in corners:

        @pl.when(ends[s, r])
        def _(s=s, r=r):
            along_y(s, r, edge).start()

        @pl.when(alone[s, r])
        def _(s=s, r=r):
            along_x(s, r, edge, False).start()

    send_faces(2)

    def arrived_y(s, r):
        along_y(s, 1 - r, edge).wait_recv()

    def arrived_x(s, r):
        along_x(1 - s, 1 - r, edge, True).wait_recv()

    for s, r in corners:

        @pl.when(middle[s, r])
        def _(s=s, r=r):
            k = 2 * s + r
            arrived_y(s, r)
            send_x[k] = edge_y[k] + edge[k]
            along_x(s, r, send_x, True).start()

    send_faces(0)

    for s, r in corners:

        @pl.when(middle[s, r])
        def _(s=s, r=r):
            k = 2 * s + r
            arrived_x(s, r)
            send_y[k] = edge_x[k] + edge[k]
            along_y(s, r, send_y).start()

    send_faces(3)

    for s, r in corners:

        @pl.when(ends[s, r])
        def _(s=s, r=r):
            arrived_y(s, r)

        @pl.when(alone[s, r])
        def _(s=s, r=r):
            arrived_x(s, r)

    transverse = lax.broadcasted_iota(jnp.int32, (8, LANES), 0)
    inner = (transverse > 0) & (transverse < 7)

    def finish(ch):
        for s in range(2):

            @pl.when(has_x[s])
            def _(s=s):
                x_copy(1 - s, ch).wait_recv()

            @pl.when(has_y[s])
            def _(s=s):
                y_copy(1 - s, ch).wait_recv()

        for s, r in corners:
            k, first = 2 * s + r, 4 + 84 * r
            part = slice(12 * ch, 12 * ch + 12)
            rx[s, ch, first:first + 12, :] = edge_y[k, part, :] + edge_x[k, part, :]

        def tile(tt, carry):
            t = 4 * ch + tt
            lanes = pl.ds(pl.multiple_of(t * LANES, LANES), LANES)
            for c in range(3):
                at = pl.ds(4 + 4 * c + tt, 8, stride=12)
                for s in range(2):
                    rows = slice(64 * c + 56 * s, 64 * c + 56 * s + 8)
                    l_t[t, rows, :] = l_t[t, rows, :] + rx[s, ch, at, :]
                for s in range(2):
                    rows = pl.ds(64 * c + 7 * s, 8, stride=8)
                    l_t[t, rows, :] = l_t[t, rows, :] + jnp.where(inner, ry[s, ch, at, :], 0.0)
            o_ref[:, lanes] = l_t[t]
            return carry

        lax.fori_loop(0, 4, tile, 0)

    for ch in (1, 2, 0, 3):
        finish(ch)

    for s in range(2):
        for ch in range(4):

            @pl.when(has_x[s])
            def _(s=s, ch=ch):
                x_copy(s, ch).wait_send()

            @pl.when(has_y[s])
            def _(s=s, ch=ch):
                y_copy(s, ch).wait_send()

    for s, r in corners:

        @pl.when(has_y[r])
        def _(s=s, r=r):
            along_y(s, r, edge).wait_send()

        @pl.when(middle[s, r] | alone[s, r])
        def _(s=s, r=r):
            along_x(s, r, edge, True).wait_send()


def third_direction_kernel(x_ref, o_hbm, out, sem):
    lane = lax.broadcasted_iota(jnp.int32, (8, out.shape[1]), 1)
    point = lane % 8
    last = out.shape[1] - 1
    top = (point == 7) & (lane != last)
    bottom = (point == 0) & (lane != 0)

    def copy(i):
        rows = pl.ds(pl.multiple_of(i * 8, 8), 8)
        return pltpu.make_async_copy(out.at[rows], o_hbm.at[rows], sem.at[i])

    def step(i, carry):
        rows = pl.ds(pl.multiple_of(i * 8, 8), 8)
        v = x_ref[rows, :]
        above = pltpu.roll(v, last, 1)
        below = pltpu.roll(v, 1, 1)
        out[rows, :] = v + jnp.where(top, above, jnp.where(bottom, below, 0.0))
        copy(i).start()
        return carry

    count = out.shape[0] // 8
    lax.fori_loop(0, count, step, 0)

    def drain(i, carry):
        copy(i).wait()
        return carry

    lax.fori_loop(0, count, drain, 0)


def solution(mesh):
    sizes = (mesh.shape["gx"], mesh.shape["gy"], mesh.shape["gz"])

    def local(values, geometry):
        tables = jnp.asarray(np.stack([lane_table(DERIVATIVE.T), lane_table(DERIVATIVE)]))
        rows, length = 192, values.shape[3]
        vmem = pl.BlockSpec(memory_space=pltpu.VMEM)
        anywhere = pl.BlockSpec(memory_space=pl.ANY)
        dma = pltpu.SemaphoreType.DMA
        summed = pl.pallas_call(
            functools.partial(exchange_kernel, sizes),
            name="exchange",
            out_shape=jax.ShapeDtypeStruct((rows, length), F32),
            in_specs=[anywhere, vmem, anywhere],
            out_specs=vmem,
            scratch_shapes=[
                pltpu.VMEM((16, rows, LANES), F32),
                pltpu.VMEM((16, rows, LANES), F32),
                pltpu.VMEM((2, 256, 256), BF16),
                pltpu.VMEM((16, 48, LANES), F32),
            ]
            + [pltpu.VMEM((rows, LANES), F32)] * 4
            + [pltpu.VMEM((2, 4, 104, LANES), F32)] * 4
            + [pltpu.VMEM((2, rows, LANES), F32)]
            + [pltpu.VMEM((4, 48, LANES), F32)] * 5
            + [dma((16,)), dma(())]
            + [dma((2, 4))] * 4
            + [dma((2,))] * 2
            + [dma((4,))] * 4,
            compiler_params=pltpu.CompilerParams(collective_id=0, has_side_effects=True),
        )(values.reshape(rows, length), geometry, tables)
        out = pl.pallas_call(
            third_direction_kernel,
            name="third",
            out_shape=jax.ShapeDtypeStruct((rows, length), F32),
            in_specs=[vmem],
            out_specs=anywhere,
            scratch_shapes=[pltpu.VMEM((rows, length), F32), dma((rows // 8,))],
        )(summed)
        return out.reshape(values.shape)

    return jax.shard_map(
        local,
        mesh=mesh,
        in_specs=(P(None, "gx", "gy", "gz"), P(None, "gx", "gy", "gz")),
        out_specs=P(None, "gx", "gy", "gz"),
        check_vma=False,
    )
```

time: 80.9 us -> 33.1 us (0.41)
  the two profiles are of different devices: /device:TPU:442 before, /device:TPU:198 now
where the time goes in v1:
time: 33.1 us; the launch traced here: 32.9 us
  Pallas kernels  32.9 us (99%)
    pallas_call x1, Pallas kernels, local(): pl.pallas_call(functools.partial(exchange_kernel, sizes), name='exchange'...  28.2 us
    pallas_call x1, Pallas kernels, local(): pl.pallas_call(third_direction_kernel, name='third', out_shape=jax.ShapeD...  4.76 us

profile of v1, /device:TPU:198, one launch (start us, length us, event | category | flops | bytes accessed | tf_op | source)
XLA Modules:
  0.0 32.9 jit_solution(18021880646065069137)
XLA Ops:
  0.0 28.2 %exchange.1.x_ref = f32[192,2048]{1,0:T(8,128)} custom-call(f32[192,2048]{1,0:T(8,128)} %bitcast.2, f32[6,1,1,256]{3,2,1,0:T(1,128)} %g_ref.1, bf16[2,256,256]{2,1,0:T(8,128)(2,1)} %constant.2.clone.tables_hbm), custom_call_target="tpu_custom_call" | custom-call | tf_op jit(solution)/shard_map/exchange/pallas_call | solution.py:475
  28.2 4.8 %third.1 = f32[192,2048]{1,0:T(8,128)} custom-call(f32[192,2048]{1,0:T(8,128)} %exchange.1.x_ref), custom_call_target="tpu_custom_call" | custom-call | tf_op jit(solution)/shard_map/third/pallas_call | solution.py:497

commit v2 on v1

--- a/solution.py
+++ b/solution.py
@@ -105,10 +105,10 @@
 
 def exchange_kernel(
     sizes,
-    u_hbm, g_ref, tables_hbm, o_ref,
-    u_t, l_t, tab, geo, s_gy, s_gz, s_fy, s_fz,
-    xf, yf, rx, ry, zr, edge, edge_y, edge_x, send_y, send_x,
-    in_sem, tab_sem, xs, xr, ys, yr, zs, zrs, eys, eyr, exs, exr,
+    u_hbm, g_hbm, tables_hbm, o_ref,
+    g_ref, u_t, l_t, tab, geo, s_gy, s_gz, s_fy, s_fz,
+    xf, yf, rx, ry, zr, edge, edge_y, edge_x, edge_d, send_y,
+    g_sem, in_sem, tab_sem, xs, xr, ys, yr, zs, zrs, eys, eyr, exs, exr, eds, edr,
 ):
     nx, ny, nz = sizes
     ix, iy, iz = lax.axis_index("gx"), lax.axis_index("gy"), lax.axis_index("gz")
@@ -127,6 +127,8 @@
 
     tile_order = [4, 5, 6, 7, 0, 15, 8, 9, 10, 11, 1, 2, 3, 12, 13, 14]
     table_copy = pltpu.make_async_copy(tables_hbm, tab, tab_sem)
+    geometry_copy = pltpu.make_async_copy(g_hbm, g_ref, g_sem)
+    geometry_copy.start()
     load(tile_order[0]).start()
     table_copy.start()
     for t in tile_order[1:]:
@@ -151,6 +153,7 @@
     sub = lax.broadcasted_iota(jnp.int32, (8, LANES), 0)
     lane = lax.broadcasted_iota(jnp.int32, (8, LANES), 1)
     plane_weight = weight_vector(sub) * weight_vector(lane)
+    geometry_copy.wait()
     for half in range(2):
         for k in range(6):
             row = jnp.broadcast_to(g_ref[k, 0, :, half * LANES:(half + 1) * LANES], (8, LANES))
@@ -178,6 +181,10 @@
             @pl.when(no_x[s] | ((parity != s) & has_y[r]))
             def _(corner=corner):
                 edge_x[corner] = jnp.zeros(edge_x.shape[1:], F32)
+
+            @pl.when(no_x[s] | (parity != s) | no_y[r])
+            def _(corner=corner):
+                edge_d[corner] = jnp.zeros(edge_d.shape[1:], F32)
 
     def compute(t):
         s_gz[...] = lane_apply(u_t[t], tab[0])
@@ -272,6 +279,10 @@
             pl.semaphore_wait(barrier, sum(there.astype(jnp.int32) for there, _ in greet))
             send_faces(1)
 
+        @pl.when(i == 9)
+        def _():
+            send_faces(2)
+
         @pl.when(i == 5)
         def _():
             for s in range(2):
@@ -308,70 +319,63 @@
             device_id={"gy": iy + step_of[r]}, device_id_type=MESH,
         )
 
-    def along_x(s, r, buf, diagonal):
-        k, there = 2 * s + r, 2 * (1 - s) + (1 - r if diagonal else r)
-        device = {"gx": ix + step_of[s]}
-        if diagonal:
-            device["gy"] = iy + step_of[r]
+    def along_x(s, r):
+        k, there = 2 * s + r, 2 * (1 - s) + r
         return pltpu.make_async_remote_copy(
-            src_ref=buf.at[k], dst_ref=edge_x.at[there], send_sem=exs.at[k], recv_sem=exr.at[there],
-            device_id=device, device_id_type=MESH,
+            src_ref=edge.at[k], dst_ref=edge_x.at[there], send_sem=exs.at[k], recv_sem=exr.at[there],
+            device_id={"gx": ix + step_of[s]}, device_id_type=MESH,
+        )
+
+    def across(s, r):
+        k, there = 2 * s + r, 2 * (1 - s) + 1 - r
+        return pltpu.make_async_remote_copy(
+            src_ref=edge.at[k], dst_ref=edge_d.at[there], send_sem=eds.at[k], recv_sem=edr.at[there],
+            device_id={"gx": ix + step_of[s], "gy": iy + step_of[r]}, device_id_type=MESH,
         )
 
     corners = [(s, r) for s in range(2) for r in range(2)]
-    middle = {(s, r): mid_x[s] & has_y[r] for s, r in corners}
-    ends = {(s, r): has_y[r] & ((parity != s) | no_x[s]) for s, r in corners}
+    inner_one = {(s, r): mid_x[s] & has_y[r] for s, r in corners}
+    outer_one = {(s, r): has_y[r] & ((parity != s) | no_x[s]) for s, r in corners}
     alone = {(s, r): has_x[s] & no_y[r] for s, r in corners}
+    send_x = {(s, r): has_x[s] & (no_y[r] | (parity != s)) for s, r in corners}
 
     for s, r in corners:
 
-        @pl.when(ends[s, r])
+        @pl.when(outer_one[s, r])
         def _(s=s, r=r):
             along_y(s, r, edge).start()
 
+        @pl.when(send_x[s, r])
+        def _(s=s, r=r):
+            along_x(s, r).start()
+
+        @pl.when(inner_one[s, r])
+        def _(s=s, r=r):
+            across(s, r).start()
+
+    send_faces(0)
+
+    for s, r in corners:
+
+        @pl.when(inner_one[s, r])
+        def _(s=s, r=r):
+            k = 2 * s + r
+            along_x(1 - s, r).wait_recv()
+            across(1 - s, 1 - r).wait_recv()
+            send_y[k] = edge_x[k] + edge_d[k] + edge[k]
+            along_y(s, r, send_y).start()
+
+    send_faces(3)
+
+    for s, r in corners:
+
+        @pl.when(has_y[r])
+        def _(s=s, r=r):
+            along_y(s, 1 - r, edge).wait_recv()
+
         @pl.when(alone[s, r])
         def _(s=s, r=r):
-            along_x(s, r, edge, False).start()
-
-    send_faces(2)
-
-    def arrived_y(s, r):
-        along_y(s, 1 - r, edge).wait_recv()
-
-    def arrived_x(s, r):
-        along_x(1 - s, 1 - r, edge, True).wait_recv()
-
-    for s, r in corners:
-
-        @pl.when(middle[s, r])
-        def _(s=s, r=r):
-            k = 2 * s + r
-            arrived_y(s, r)
-            send_x[k] = edge_y[k] + edge[k]
-            along_x(s, r, send_x, True).start()
-
-    send_faces(0)
-
-    for s, r in corners:
-
-        @pl.when(middle[s, r])
-        def _(s=s, r=r):
-            k = 2 * s + r
-            arrived_x(s, r)
-            send_y[k] = edge_x[k] + edge[k]
-            along_y(s, r, send_y).start()
-
-    send_faces(3)
-
-    for s, r in corners:
-
-        @pl.when(ends[s, r])
-        def _(s=s, r=r):
-            arrived_y(s, r)
-
-        @pl.when(alone[s, r])
-        def _(s=s, r=r):
-            arrived_x(s, r)
+            along_x(1 - s, r).wait_recv()
 
     transverse = lax.broadcasted_iota(jnp.int32, (8, LANES), 0)
     inner = (transverse > 0) & (transverse < 7)
@@ -390,7 +394,7 @@
         for s, r in corners:
             k, first = 2 * s + r, 4 + 84 * r
             part = slice(12 * ch, 12 * ch + 12)
-            rx[s, ch, first:first + 12, :] = edge_y[k, part, :] + edge_x[k, part, :]
+            rx[s, ch, first:first + 12, :] = edge_y[k, part, :] + edge_x[k, part, :] + edge_d[k, part, :]
 
         def tile(tt, carry):
             t = 4 * ch + tt
@@ -428,9 +432,13 @@
         def _(s=s, r=r):
             along_y(s, r, edge).wait_send()
 
-        @pl.when(middle[s, r] | alone[s, r])
-        def _(s=s, r=r):
-            along_x(s, r, edge, True).wait_send()
+        @pl.when(send_x[s, r])
+        def _(s=s, r=r):
+            along_x(s, r).wait_send()
+
+        @pl.when(inner_one[s, r])
+        def _(s=s, r=r):
+            across(s, r).wait_send()
 
 
 def third_direction_kernel(x_ref, o_hbm, out, sem):
@@ -441,11 +449,11 @@
     bottom = (point == 0) & (lane != 0)
 
     def copy(i):
-        rows = pl.ds(pl.multiple_of(i * 8, 8), 8)
+        rows = pl.ds(i * 8 if isinstance(i, int) else pl.multiple_of(i * 8, 8), 8)
         return pltpu.make_async_copy(out.at[rows], o_hbm.at[rows], sem.at[i])
 
     def step(i, carry):
-        rows = pl.ds(pl.multiple_of(i * 8, 8), 8)
+        rows = pl.ds(i * 8, 8)
         v = x_ref[rows, :]
         above = pltpu.roll(v, last, 1)
         below = pltpu.roll(v, 1, 1)
@@ -454,7 +462,8 @@
         return carry
 
     count = out.shape[0] // 8
-    lax.fori_loop(0, count, step, 0)
+    for i in range(count):
+        step(i, 0)
 
     def drain(i, carry):
         copy(i).wait()
@@ -470,15 +479,16 @@
         tables = jnp.asarray(np.stack([lane_table(DERIVATIVE.T), lane_table(DERIVATIVE)]))
         rows, length = 192, values.shape[3]
         vmem = pl.BlockSpec(memory_space=pltpu.VMEM)
-        anywhere = pl.BlockSpec(memory_space=pl.ANY)
+        hbm = pl.BlockSpec(memory_space=pltpu.HBM)
         dma = pltpu.SemaphoreType.DMA
         summed = pl.pallas_call(
             functools.partial(exchange_kernel, sizes),
             name="exchange",
-            out_shape=jax.ShapeDtypeStruct((rows, length), F32),
-            in_specs=[anywhere, vmem, anywhere],
+            out_shape=pltpu.VMEM((rows, length), F32),
+            in_specs=[hbm, hbm, hbm],
             out_specs=vmem,
             scratch_shapes=[
+                pltpu.VMEM(geometry.shape, F32),
                 pltpu.VMEM((16, rows, LANES), F32),
                 pltpu.VMEM((16, rows, LANES), F32),
                 pltpu.VMEM((2, 256, 256), BF16),
@@ -488,19 +498,24 @@
             + [pltpu.VMEM((2, 4, 104, LANES), F32)] * 4
             + [pltpu.VMEM((2, rows, LANES), F32)]
             + [pltpu.VMEM((4, 48, LANES), F32)] * 5
-            + [dma((16,)), dma(())]
+            + [dma(()), dma((16,)), dma(())]
             + [dma((2, 4))] * 4
             + [dma((2,))] * 2
-            + [dma((4,))] * 4,
-            compiler_params=pltpu.CompilerParams(collective_id=0, has_side_effects=True),
-        )(values.reshape(rows, length), geometry, tables)
+            + [dma((4,))] * 6,
+            compiler_params=pltpu.CompilerParams(collective_id=0, has_side_effects=True, vmem_limit_bytes=16 << 20),
+        )(
+            pltpu.with_memory_space_constraint(values.reshape(rows, length), pltpu.HBM),
+            pltpu.with_memory_space_constraint(geometry, pltpu.HBM),
+            pltpu.with_memory_space_constraint(tables, pltpu.HBM),
+        )
         out = pl.pallas_call(
             third_direction_kernel,
             name="third",
             out_shape=jax.ShapeDtypeStruct((rows, length), F32),
             in_specs=[vmem],
-            out_specs=anywhere,
+            out_specs=hbm,
             scratch_shapes=[pltpu.VMEM((rows, length), F32), dma((rows // 8,))],
+            compiler_params=pltpu.CompilerParams(vmem_limit_bytes=8 << 20),
         )(summed)
         return out.reshape(values.shape)
 

time: 33.1 us -> 27 us (0.82)
  the two profiles are of different devices: /device:TPU:198 before, /device:TPU:204 now
where the time goes in v2:
time: 27 us; the launch traced here: 26.9 us
  Pallas kernels  26.9 us (100%)
    pallas_call x1, Pallas kernels, local(): pl.pallas_call(functools.partial(exchange_kernel, sizes), name='exchange'...  25.2 us
    pallas_call x1, Pallas kernels, local(): pl.pallas_call(third_direction_kernel, name='third', out_shape=jax.ShapeD...  1.72 us

profile of v2, /device:TPU:204, one launch (start us, length us, event | category | flops | bytes accessed | tf_op | source)
XLA Modules:
  0.0 26.9 jit_solution(6288303510334186463)
XLA Ops:
  0.0 25.2 %exchange.1.x_ref = f32[192,2048]{1,0:T(8,128)S(1)} custom-call(f32[192,2048]{1,0:T(8,128)} %bitcast.2, f32[6,1,1,256]{3,2,1,0:T(1,128)} %g_hbm.1, bf16[2,256,256]{2,1,0:T(8,128)(2,1)} %constant.2.clone.tables_hbm), custom_call_target="tpu_custom_call" | custom-call | tf_op jit(solution)/shard_map/exchange/pallas_call | solution.py:484
  25.2 1.7 %third.1 = f32[192,2048]{1,0:T(8,128)} custom-call(f32[192,2048]{1,0:T(8,128)S(1)} %exchange.1.x_ref), custom_call_target="tpu_custom_call" | custom-call | tf_op jit(solution)/shard_map/third/pallas_call | solution.py:511

commit v3 on v2

--- a/solution.py
+++ b/solution.py
@@ -106,8 +106,8 @@
 def exchange_kernel(
     sizes,
     u_hbm, g_hbm, tables_hbm, o_ref,
-    g_ref, u_t, l_t, tab, geo, s_gy, s_gz, s_fy, s_fz,
-    xf, yf, rx, ry, zr, edge, edge_y, edge_x, edge_d, send_y,
+    g_ref, u_t, l_t, tab, geo, s_gy, s_gz, s_fy, s_fz, s_ox,
+    xf, yf, rx, ry, zr, edge, edge_y, edge_x, edge_d, passed,
     g_sem, in_sem, tab_sem, xs, xr, ys, yr, zs, zrs, eys, eyr, exs, exr, eds, edr,
 ):
     nx, ny, nz = sizes
@@ -125,15 +125,6 @@
             u_hbm.at[:, pl.ds(pl.multiple_of(t * LANES, LANES), LANES)], u_t.at[t], in_sem.at[t]
         )
 
-    tile_order = [4, 5, 6, 7, 0, 15, 8, 9, 10, 11, 1, 2, 3, 12, 13, 14]
-    table_copy = pltpu.make_async_copy(tables_hbm, tab, tab_sem)
-    geometry_copy = pltpu.make_async_copy(g_hbm, g_ref, g_sem)
-    geometry_copy.start()
-    load(tile_order[0]).start()
-    table_copy.start()
-    for t in tile_order[1:]:
-        load(t).start()
-
     barrier = pltpu.get_barrier_semaphore()
     dxm = 2 * parity - 1
     mid_x = [(parity == s) & has_x[s] for s in range(2)]
@@ -150,6 +141,15 @@
         def _(device=device):
             pl.semaphore_signal(barrier, inc=1, device_id=device, device_id_type=MESH)
 
+    tile_order = [4, 5, 6, 7, 0, 15, 8, 9, 10, 11, 1, 2, 3, 12, 13, 14]
+    table_copy = pltpu.make_async_copy(tables_hbm, tab, tab_sem)
+    geometry_copy = pltpu.make_async_copy(g_hbm, g_ref, g_sem)
+    geometry_copy.start()
+    load(tile_order[0]).start()
+    table_copy.start()
+    for t in tile_order[1:]:
+        load(t).start()
+
     sub = lax.broadcasted_iota(jnp.int32, (8, LANES), 0)
     lane = lax.broadcasted_iota(jnp.int32, (8, LANES), 1)
     plane_weight = weight_vector(sub) * weight_vector(lane)
@@ -186,41 +186,43 @@
             def _(corner=corner):
                 edge_d[corner] = jnp.zeros(edge_d.shape[1:], F32)
 
-    def compute(t):
-        s_gz[...] = lane_apply(u_t[t], tab[0])
-        for c in range(3):
-            base = 64 * c
-            uy = [u_t[t, pl.ds(base + y, 8, stride=8), :] for y in range(8)]
-            gy = apply_halves(GRAD, uy)
-            for y in range(8):
-                s_gy[pl.ds(base + y, 8, stride=8), :] = gy[y]
-        g00, g11, g22, g01, g02, g12 = [geo[t, 8 * k:8 * k + 8, :] for k in range(6)]
-        for c in range(3):
-            base = 64 * c
-            ux = [u_t[t, base + 8 * x:base + 8 * x + 8, :] for x in range(8)]
-            gx = apply_halves(GRAD, ux)
-            fx = []
-            for x in range(8):
-                rows = slice(base + 8 * x, base + 8 * x + 8)
-                a, b, d = gx[x], s_gy[rows, :], s_gz[rows, :]
-                fx.append(g00 * a + g01 * b + g02 * d)
-                s_fy[rows, :] = g01 * a + g11 * b + g12 * d
-                s_fz[rows, :] = g02 * a + g12 * b + g22 * d
-            ox = apply_halves(BACK_X, fx)
-            for x in range(8):
-                l_t[t, base + 8 * x:base + 8 * x + 8, :] = ox[x]
-        s_gz[...] = lane_apply(s_fz[...], tab[1])
-        for c in range(3):
-            base = 64 * c
-            fy = [s_fy[pl.ds(base + y, 8, stride=8), :] for y in range(8)]
-            oy = apply_halves(BACK, fy)
-            for y in range(8):
-                s_gy[pl.ds(base + y, 8, stride=8), :] = oy[y]
-        for c in range(3):
-            base = 64 * c
-            for x in range(8):
-                rows = slice(base + 8 * x, base + 8 * x + 8)
-                l_t[t, rows, :] = l_t[t, rows, :] + WEIGHTS[x] * (s_gy[rows, :] + s_gz[rows, :])
+    def compute(pair):
+        for p, t in enumerate(pair):
+            s_gz[p] = lane_apply(u_t[t], tab[0])
+        for p, t in enumerate(pair):
+            for c in range(3):
+                uy = [u_t[t, pl.ds(64 * c + y, 8, stride=8), :] for y in range(8)]
+                gy = apply_halves(GRAD, uy)
+                for y in range(8):
+                    s_gy[p, pl.ds(64 * c + y, 8, stride=8), :] = gy[y]
+        for p, t in enumerate(pair):
+            g00, g11, g22, g01, g02, g12 = [geo[t, 8 * k:8 * k + 8, :] for k in range(6)]
+            for c in range(3):
+                base = 64 * c
+                ux = [u_t[t, base + 8 * x:base + 8 * x + 8, :] for x in range(8)]
+                gx = apply_halves(GRAD, ux)
+                fx = []
+                for x in range(8):
+                    rows = slice(base + 8 * x, base + 8 * x + 8)
+                    a, b, d = gx[x], s_gy[p, rows, :], s_gz[p, rows, :]
+                    fx.append(g00 * a + g01 * b + g02 * d)
+                    s_fy[p, rows, :] = g01 * a + g11 * b + g12 * d
+                    s_fz[p, rows, :] = g02 * a + g12 * b + g22 * d
+                ox = apply_halves(BACK_X, fx)
+                for x in range(8):
+                    s_ox[p, base + 8 * x:base + 8 * x + 8, :] = ox[x]
+            s_gz[p] = lane_apply(s_fz[p], tab[1])
+        for p, t in enumerate(pair):
+            for c in range(3):
+                fy = [s_fy[p, pl.ds(64 * c + y, 8, stride=8), :] for y in range(8)]
+                oy = apply_halves(BACK, fy)
+                for y in range(8):
+                    s_gy[p, pl.ds(64 * c + y, 8, stride=8), :] = oy[y]
+        for p, t in enumerate(pair):
+            for c in range(3):
+                for x in range(8):
+                    rows = slice(64 * c + 8 * x, 64 * c + 8 * x + 8)
+                    l_t[t, rows, :] = s_ox[p, rows, :] + WEIGHTS[x] * (s_gy[p, rows, :] + s_gz[p, rows, :])
 
     def faces(t):
         ch, tt = t // 4, t % 4
@@ -246,16 +248,15 @@
     def y_copy(s, ch):
         return face_copy(yf, ry, ys, yr, "gy", iy, s, ch)
 
-    def send_faces(ch):
-        for s in range(2):
-
-            @pl.when(has_x[s])
-            def _(s=s):
-                x_copy(s, ch).start()
-
-            @pl.when(has_y[s])
-            def _(s=s):
-                y_copy(s, ch).start()
+    def send_x(s, ch):
+        @pl.when(has_x[s])
+        def _():
+            x_copy(s, ch).start()
+
+    def send_y(s, ch):
+        @pl.when(has_y[s])
+        def _():
+            y_copy(s, ch).start()
 
     def z_copy(s):
         return pltpu.make_async_remote_copy(
@@ -266,24 +267,30 @@
     table_copy.wait()
 
     def step(i, carry):
-        t = jnp.where(
-            i < 4, i + 4,
-            jnp.where(i < 6, (i - 4) * 15, jnp.where(i < 10, i + 2, jnp.where(i < 13, i - 9, i - 1))),
-        )
-        load(t).wait()
-        compute(t)
-        faces(t)
-
-        @pl.when(i == 3)
+        first = jnp.where(i < 2, 2 * i + 4, jnp.where(i == 2, 0, jnp.where(i < 5, 2 * i + 2, jnp.where(i < 7, 2 * i - 9, 13))))
+        second = jnp.where(i == 2, 15, jnp.where(i == 6, 12, first + 1))
+        for t in (first, second):
+            load(t).wait()
+        compute((first, second))
+        for t in (first, second):
+            faces(t)
+
+        @pl.when(i == 1)
         def _():
             pl.semaphore_wait(barrier, sum(there.astype(jnp.int32) for there, _ in greet))
-            send_faces(1)
-
-        @pl.when(i == 9)
+            send_x(0, 1)
+            send_y(0, 1)
+            send_y(1, 1)
+            send_x(1, 1)
+
+        @pl.when(i == 4)
         def _():
-            send_faces(2)
-
-        @pl.when(i == 5)
+            send_x(0, 2)
+            send_y(0, 2)
+            send_y(1, 2)
+            send_x(1, 2)
+
+        @pl.when(i == 2)
         def _():
             for s in range(2):
 
@@ -293,7 +300,7 @@
 
         return carry
 
-    lax.fori_loop(0, 16, step, 0)
+    lax.fori_loop(0, 8, step, 0)
 
     wide = lax.broadcasted_iota(jnp.int32, (192, LANES), 1)
     for s in range(2):
@@ -337,45 +344,7 @@
     inner_one = {(s, r): mid_x[s] & has_y[r] for s, r in corners}
     outer_one = {(s, r): has_y[r] & ((parity != s) | no_x[s]) for s, r in corners}
     alone = {(s, r): has_x[s] & no_y[r] for s, r in corners}
-    send_x = {(s, r): has_x[s] & (no_y[r] | (parity != s)) for s, r in corners}
-
-    for s, r in corners:
-
-        @pl.when(outer_one[s, r])
-        def _(s=s, r=r):
-            along_y(s, r, edge).start()
-
-        @pl.when(send_x[s, r])
-        def _(s=s, r=r):
-            along_x(s, r).start()
-
-        @pl.when(inner_one[s, r])
-        def _(s=s, r=r):
-            across(s, r).start()
-
-    send_faces(0)
-
-    for s, r in corners:
-
-        @pl.when(inner_one[s, r])
-        def _(s=s, r=r):
-            k = 2 * s + r
-            along_x(1 - s, r).wait_recv()
-            across(1 - s, 1 - r).wait_recv()
-            send_y[k] = edge_x[k] + edge_d[k] + edge[k]
-            along_y(s, r, send_y).start()
-
-    send_faces(3)
-
-    for s, r in corners:
-
-        @pl.when(has_y[r])
-        def _(s=s, r=r):
-            along_y(s, 1 - r, edge).wait_recv()
-
-        @pl.when(alone[s, r])
-        def _(s=s, r=r):
-            along_x(1 - s, r).wait_recv()
+    cross_x = {(s, r): has_x[s] & (no_y[r] | (parity != s)) for s, r in corners}
 
     transverse = lax.broadcasted_iota(jnp.int32, (8, LANES), 0)
     inner = (transverse > 0) & (transverse < 7)
@@ -390,11 +359,6 @@
             @pl.when(has_y[s])
             def _(s=s):
                 y_copy(1 - s, ch).wait_recv()
-
-        for s, r in corners:
-            k, first = 2 * s + r, 4 + 84 * r
-            part = slice(12 * ch, 12 * ch + 12)
-            rx[s, ch, first:first + 12, :] = edge_y[k, part, :] + edge_x[k, part, :] + edge_d[k, part, :]
 
         def tile(tt, carry):
             t = 4 * ch + tt
@@ -403,7 +367,7 @@
                 at = pl.ds(4 + 4 * c + tt, 8, stride=12)
                 for s in range(2):
                     rows = slice(64 * c + 56 * s, 64 * c + 56 * s + 8)
-                    l_t[t, rows, :] = l_t[t, rows, :] + rx[s, ch, at, :]
+                    l_t[t, rows, :] = l_t[t, rows, :] + jnp.where(inner, rx[s, ch, at, :], 0.0)
                 for s in range(2):
                     rows = pl.ds(64 * c + 7 * s, 8, stride=8)
                     l_t[t, rows, :] = l_t[t, rows, :] + jnp.where(inner, ry[s, ch, at, :], 0.0)
@@ -412,27 +376,112 @@
 
         lax.fori_loop(0, 4, tile, 0)
 
-    for ch in (1, 2, 0, 3):
-        finish(ch)
-
-    for s in range(2):
-        for ch in range(4):
+    def finish_edges():
+        for s, r in corners:
+            k, first = 2 * s + r, 4 + 84 * r
+            for ch in range(4):
+                part = slice(12 * ch, 12 * ch + 12)
+                xf[s, ch, first:first + 12, :] = edge_y[k, part, :] + edge_x[k, part, :] + edge_d[k, part, :]
+
+        def rows_of(t):
+            for c in range(3):
+                at = pl.ds(4 + 4 * c + t % 4, 8, stride=12)
+                for s in range(2):
+                    rows = slice(64 * c + 56 * s, 64 * c + 56 * s + 8)
+                    yield rows, jnp.where(inner, 0.0, xf[s, t // 4, at, :])
+
+        def done(t, carry):
+            lanes = pl.ds(pl.multiple_of(t * LANES, LANES), LANES)
+            for rows, term in rows_of(t):
+                o_ref[rows, lanes] = o_ref[rows, lanes] + term
+            return carry
+
+        def pending(t, carry):
+            for rows, term in rows_of(t):
+                l_t[t, rows, :] = l_t[t, rows, :] + term
+            return carry
+
+        lax.fori_loop(0, 12, done, 0, unroll=2)
+        lax.fori_loop(12, 16, pending, 0, unroll=2)
+
+    def sent(ch):
+        for s in range(2):
 
             @pl.when(has_x[s])
-            def _(s=s, ch=ch):
+            def _(s=s):
                 x_copy(s, ch).wait_send()
 
             @pl.when(has_y[s])
-            def _(s=s, ch=ch):
+            def _(s=s):
                 y_copy(s, ch).wait_send()
 
     for s, r in corners:
 
+        @pl.when(outer_one[s, r])
+        def _(s=s, r=r):
+            along_y(s, r, edge).start()
+
+        @pl.when(cross_x[s, r])
+        def _(s=s, r=r):
+            along_x(s, r).start()
+
+        @pl.when(inner_one[s, r])
+        def _(s=s, r=r):
+            across(s, r).start()
+
+    send_x(0, 0)
+
+    send_x(0, 3)
+
+    send_y(0, 0)
+    send_y(1, 0)
+
+    send_x(1, 0)
+
+    for s, r in corners:
+
+        @pl.when(inner_one[s, r])
+        def _(s=s, r=r):
+            k = 2 * s + r
+            along_x(1 - s, r).wait_recv()
+            across(1 - s, 1 - r).wait_recv()
+            passed[k] = edge_x[k] + edge_d[k] + edge[k]
+            along_y(s, r, passed).start()
+
+    send_y(0, 3)
+    send_y(1, 3)
+
+    send_x(1, 3)
+
+    finish(1)
+
+    finish(2)
+
+    sent(1)
+
+    sent(2)
+
+    finish(0)
+
+    sent(0)
+
+    for s, r in corners:
+
         @pl.when(has_y[r])
         def _(s=s, r=r):
+            along_y(s, 1 - r, edge).wait_recv()
+
+        @pl.when(alone[s, r])
+        def _(s=s, r=r):
+            along_x(1 - s, r).wait_recv()
+
+    for s, r in corners:
+
+        @pl.when(has_y[r])
+        def _(s=s, r=r):
             along_y(s, r, edge).wait_send()
 
-        @pl.when(send_x[s, r])
+        @pl.when(cross_x[s, r])
         def _(s=s, r=r):
             along_x(s, r).wait_send()
 
@@ -440,36 +489,42 @@
         def _(s=s, r=r):
             across(s, r).wait_send()
 
+    finish_edges()
+
+    finish(3)
+
+    sent(3)
+
 
 def third_direction_kernel(x_ref, o_hbm, out, sem):
-    lane = lax.broadcasted_iota(jnp.int32, (8, out.shape[1]), 1)
+    tiles = out.shape[1] // LANES
+    lane = lax.broadcasted_iota(jnp.int32, (8, LANES), 1)
     point = lane % 8
-    last = out.shape[1] - 1
-    top = (point == 7) & (lane != last)
-    bottom = (point == 0) & (lane != 0)
+    shared = (point == 7) | (point == 0)
+    swap = jnp.where(point == 7, (lane + 1) % LANES, jnp.where(point == 0, (lane + LANES - 1) % LANES, lane))
+    head, tail = lane == 0, lane == LANES - 1
+    first, last = shared & (lane > 0), shared & (lane < LANES - 1)
 
     def copy(i):
-        rows = pl.ds(i * 8 if isinstance(i, int) else pl.multiple_of(i * 8, 8), 8)
+        rows = pl.ds(8 * i, 8)
         return pltpu.make_async_copy(out.at[rows], o_hbm.at[rows], sem.at[i])
-
-    def step(i, carry):
-        rows = pl.ds(i * 8, 8)
-        v = x_ref[rows, :]
-        above = pltpu.roll(v, last, 1)
-        below = pltpu.roll(v, 1, 1)
-        out[rows, :] = v + jnp.where(top, above, jnp.where(bottom, below, 0.0))
-        copy(i).start()
-        return carry
 
     count = out.shape[0] // 8
     for i in range(count):
-        step(i, 0)
-
-    def drain(i, carry):
+        rows = slice(8 * i, 8 * i + 8)
+        own = [x_ref[rows, LANES * t:LANES * (t + 1)] for t in range(tiles)]
+        other = [jnp.take_along_axis(v, swap, axis=1) for v in own]
+        for t in range(tiles):
+            take = other[t]
+            if t > 0:
+                take = jnp.where(head, other[t - 1], take)
+            if t < tiles - 1:
+                take = jnp.where(tail, other[t + 1], take)
+            mask = first if t == 0 else last if t == tiles - 1 else shared
+            out[rows, LANES * t:LANES * (t + 1)] = own[t] + jnp.where(mask, take, 0.0)
+        copy(i).start()
+    for i in range(count):
         copy(i).wait()
-        return carry
-
-    lax.fori_loop(0, count, drain, 0)
 
 
 def solution(mesh):
@@ -494,7 +549,7 @@
                 pltpu.VMEM((2, 256, 256), BF16),
                 pltpu.VMEM((16, 48, LANES), F32),
             ]
-            + [pltpu.VMEM((rows, LANES), F32)] * 4
+            + [pltpu.VMEM((2, rows, LANES), F32)] * 5
             + [pltpu.VMEM((2, 4, 104, LANES), F32)] * 4
             + [pltpu.VMEM((2, rows, LANES), F32)]
             + [pltpu.VMEM((4, 48, LANES), F32)] * 5

time: 27 us -> 26.1 us (0.967)
  the two profiles are of different devices: /device:TPU:204 before, /device:TPU:198 now
where the time goes in v3:
time: 26.1 us; the launch traced here: 25.9 us
  Pallas kernels  25.9 us (99%)
    pallas_call x1, Pallas kernels, local(): pl.pallas_call(functools.partial(exchange_kernel, sizes), name='exchange'...  24.5 us
    pallas_call x1, Pallas kernels, local(): pl.pallas_call(third_direction_kernel, name='third', out_shape=jax.ShapeD...  1.42 us

profile of v3, /device:TPU:198, one launch (start us, length us, event | category | flops | bytes accessed | tf_op | source)
XLA Modules:
  0.0 25.9 jit_solution(9720438683227552985)
XLA Ops:
  0.0 24.5 %exchange.1.x_ref = f32[192,2048]{1,0:T(8,128)S(1)} custom-call(f32[192,2048]{1,0:T(8,128)} %bitcast.2, f32[6,1,1,256]{3,2,1,0:T(1,128)} %g_hbm.1, bf16[2,256,256]{2,1,0:T(8,128)(2,1)} %constant.2.clone.tables_hbm), custom_call_target="tpu_custom_call" | custom-call | tf_op jit(solution)/shard_map/exchange/pallas_call | solution.py:539
  24.5 1.4 %third.1 = f32[192,2048]{1,0:T(8,128)} custom-call(f32[192,2048]{1,0:T(8,128)S(1)} %exchange.1.x_ref), custom_call_target="tpu_custom_call" | custom-call | tf_op jit(solution)/shard_map/third/pallas_call | solution.py:566

commit v4 on v3

--- a/solution.py
+++ b/solution.py
@@ -161,6 +161,15 @@
                 picked = jnp.take_along_axis(row, lane // 8 + 16 * j, axis=1)
                 geo[half * 8 + j, 8 * k:8 * k + 8, :] = picked * plane_weight
 
+    even, odd = parity == 0, parity == 1
+    corners = [(s, r) for s in range(2) for r in range(2)]
+    hub = [has_x[0] & has_y[r] & even for r in range(2)]
+    use_y = {(s, r): has_y[r] if s == 0 else has_y[r] & no_x[s] for s, r in corners}
+    use_x = {(s, r): has_x[s] & (no_y[r] | even) for s, r in corners}
+    use_d = {(s, r): has_x[s] & has_y[r] & (even if s == 0 else odd) for s, r in corners}
+    early_y = {(s, r): has_y[r] & (no_x[s] | odd) if s == 0 else use_y[s, r] for s, r in corners}
+    early_x = {(s, r): has_x[s] & no_y[r] if s == 0 else use_x[s, r] for s, r in corners}
+
     for s in range(2):
 
         @pl.when(no_x[s])
@@ -171,20 +180,13 @@
         def _(s=s):
             ry[s] = jnp.zeros(ry.shape[1:], F32)
 
-        for r in range(2):
-            corner = 2 * s + r
-
-            @pl.when(no_y[r])
-            def _(corner=corner):
-                edge_y[corner] = jnp.zeros(edge_y.shape[1:], F32)
-
-            @pl.when(no_x[s] | ((parity != s) & has_y[r]))
-            def _(corner=corner):
-                edge_x[corner] = jnp.zeros(edge_x.shape[1:], F32)
-
-            @pl.when(no_x[s] | (parity != s) | no_y[r])
-            def _(corner=corner):
-                edge_d[corner] = jnp.zeros(edge_d.shape[1:], F32)
+    for s, r in corners:
+        k = 2 * s + r
+        for used, land in ((use_y, edge_y), (use_x, edge_x), (use_d, edge_d)):
+
+            @pl.when(jnp.logical_not(used[s, r]))
+            def _(k=k, land=land):
+                land[k] = jnp.zeros(land.shape[1:], F32)
 
     def compute(pair):
         for p, t in enumerate(pair):
@@ -313,38 +315,32 @@
             l_t[15 * s] = l_t[15 * s] + jnp.where(wide == (LANES - 1) * s, landed, 0.0)
             faces(15 * s)
 
-    for s in range(2):
-        for r in range(2):
-            for ch in range(4):
-                first = 4 + 84 * r
-                edge[2 * s + r, 12 * ch:12 * ch + 12, :] = xf[s, ch, first:first + 12, :]
-
-    def along_y(s, r, buf):
-        k, there = 2 * s + r, 2 * s + 1 - r
+    for s, r in corners:
+        for ch in range(4):
+            first = 4 + 84 * r
+            edge[2 * s + r, 12 * ch:12 * ch + 12, :] = xf[s, ch, first:first + 12, :]
+
+    def edge_copy(s, r, src, land, send, recv, dx, dy):
+        k = 2 * s + r
+        there = 2 * (1 - s if dx else s) + (1 - r if dy else r)
+        device = {}
+        if dx:
+            device["gx"] = ix + step_of[s]
+        if dy:
+            device["gy"] = iy + step_of[r]
         return pltpu.make_async_remote_copy(
-            src_ref=buf.at[k], dst_ref=edge_y.at[there], send_sem=eys.at[k], recv_sem=eyr.at[there],
-            device_id={"gy": iy + step_of[r]}, device_id_type=MESH,
+            src_ref=src, dst_ref=land.at[there], send_sem=send.at[k], recv_sem=recv.at[there],
+            device_id=device, device_id_type=MESH,
         )
 
-    def along_x(s, r):
-        k, there = 2 * s + r, 2 * (1 - s) + r
-        return pltpu.make_async_remote_copy(
-            src_ref=edge.at[k], dst_ref=edge_x.at[there], send_sem=exs.at[k], recv_sem=exr.at[there],
-            device_id={"gx": ix + step_of[s]}, device_id_type=MESH,
-        )
-
-    def across(s, r):
-        k, there = 2 * s + r, 2 * (1 - s) + 1 - r
-        return pltpu.make_async_remote_copy(
-            src_ref=edge.at[k], dst_ref=edge_d.at[there], send_sem=eds.at[k], recv_sem=edr.at[there],
-            device_id={"gx": ix + step_of[s], "gy": iy + step_of[r]}, device_id_type=MESH,
-        )
-
-    corners = [(s, r) for s in range(2) for r in range(2)]
-    inner_one = {(s, r): mid_x[s] & has_y[r] for s, r in corners}
-    outer_one = {(s, r): has_y[r] & ((parity != s) | no_x[s]) for s, r in corners}
-    alone = {(s, r): has_x[s] & no_y[r] for s, r in corners}
-    cross_x = {(s, r): has_x[s] & (no_y[r] | (parity != s)) for s, r in corners}
+    def along_y(s, r, src=None):
+        return edge_copy(s, r, edge.at[2 * s + r] if src is None else src, edge_y, eys, eyr, False, True)
+
+    def along_x(s, r, src=None):
+        return edge_copy(s, r, edge.at[2 * s + r] if src is None else src, edge_x, exs, exr, True, False)
+
+    def across(s, r, src=None):
+        return edge_copy(s, r, edge.at[2 * s + r] if src is None else src, edge_d, eds, edr, True, True)
 
     transverse = lax.broadcasted_iota(jnp.int32, (8, LANES), 0)
     inner = (transverse > 0) & (transverse < 7)
@@ -417,36 +413,42 @@
 
     for s, r in corners:
 
-        @pl.when(outer_one[s, r])
-        def _(s=s, r=r):
-            along_y(s, r, edge).start()
-
-        @pl.when(cross_x[s, r])
+        @pl.when(early_y[s, r])
+        def _(s=s, r=r):
+            along_y(s, r).start()
+
+        @pl.when(early_x[s, r])
         def _(s=s, r=r):
             along_x(s, r).start()
 
-        @pl.when(inner_one[s, r])
-        def _(s=s, r=r):
-            across(s, r).start()
+        if s == 1:
+
+            @pl.when(use_d[s, r])
+            def _(s=s, r=r):
+                across(s, r).start()
 
     send_x(0, 0)
-
-    send_x(0, 3)
 
     send_y(0, 0)
     send_y(1, 0)
 
     send_x(1, 0)
 
-    for s, r in corners:
-
-        @pl.when(inner_one[s, r])
-        def _(s=s, r=r):
-            k = 2 * s + r
-            along_x(1 - s, r).wait_recv()
-            across(1 - s, 1 - r).wait_recv()
-            passed[k] = edge_x[k] + edge_d[k] + edge[k]
-            along_y(s, r, passed).start()
+    for r in (1, 0):
+
+        @pl.when(hub[r])
+        def _(r=r):
+            along_y(0, 1 - r).wait_recv()
+            across(1, 1 - r).wait_recv()
+            along_x(1, r).wait_recv()
+            passed[3 * r] = edge[r] + edge_d[r] + edge_y[r]
+            passed[3 * r + 1] = edge[r] + edge_x[r] + edge_y[r]
+            passed[3 * r + 2] = edge[r] + edge_x[r] + edge_d[r]
+            across(0, r, passed.at[3 * r + 1]).start()
+            along_x(0, r, passed.at[3 * r]).start()
+            along_y(0, r, passed.at[3 * r + 2]).start()
+
+    send_x(0, 3)
 
     send_y(0, 3)
     send_y(1, 3)
@@ -467,25 +469,31 @@
 
     for s, r in corners:
 
-        @pl.when(has_y[r])
-        def _(s=s, r=r):
-            along_y(s, 1 - r, edge).wait_recv()
-
-        @pl.when(alone[s, r])
+        @pl.when(early_y[s, r])
+        def _(s=s, r=r):
+            along_y(s, 1 - r).wait_recv()
+
+        @pl.when(early_x[s, r])
         def _(s=s, r=r):
             along_x(1 - s, r).wait_recv()
 
+        if s == 1:
+
+            @pl.when(use_d[s, r])
+            def _(s=s, r=r):
+                across(1 - s, 1 - r).wait_recv()
+
     for s, r in corners:
 
-        @pl.when(has_y[r])
-        def _(s=s, r=r):
-            along_y(s, r, edge).wait_send()
-
-        @pl.when(cross_x[s, r])
+        @pl.when(use_y[s, r])
+        def _(s=s, r=r):
+            along_y(s, r).wait_send()
+
+        @pl.when(use_x[s, r])
         def _(s=s, r=r):
             along_x(s, r).wait_send()
 
-        @pl.when(inner_one[s, r])
+        @pl.when(use_d[s, r])
         def _(s=s, r=r):
             across(s, r).wait_send()
 
@@ -552,7 +560,8 @@
             + [pltpu.VMEM((2, rows, LANES), F32)] * 5
             + [pltpu.VMEM((2, 4, 104, LANES), F32)] * 4
             + [pltpu.VMEM((2, rows, LANES), F32)]
-            + [pltpu.VMEM((4, 48, LANES), F32)] * 5
+            + [pltpu.VMEM((4, 48, LANES), F32)] * 4
+            + [pltpu.VMEM((6, 48, LANES), F32)]
             + [dma(()), dma((16,)), dma(())]
             + [dma((2, 4))] * 4
             + [dma((2,))] * 2

time: 26.1 us -> 25.7 us (0.985)
  the two profiles are of different devices: /device:TPU:198 before, /device:TPU:220 now
where the time goes in v4:
time: 25.7 us; the launch traced here: 25.5 us
  Pallas kernels  25.5 us (99%)
    pallas_call x1, Pallas kernels, local(): pl.pallas_call(functools.partial(exchange_kernel, sizes), name='exchange'...  24.1 us
    pallas_call x1, Pallas kernels, local(): pl.pallas_call(third_direction_kernel, name='third', out_shape=jax.ShapeD...  1.42 us

profile of v4, /device:TPU:220, one launch (start us, length us, event | category | flops | bytes accessed | tf_op | source)
XLA Modules:
  0.0 25.5 jit_solution(5411767883575748420)
XLA Ops:
  0.0 24.1 %exchange.1.x_ref = f32[192,2048]{1,0:T(8,128)S(1)} custom-call(f32[192,2048]{1,0:T(8,128)} %bitcast.2, f32[6,1,1,256]{3,2,1,0:T(1,128)} %g_hbm.1, bf16[2,256,256]{2,1,0:T(8,128)(2,1)} %constant.2.clone.tables_hbm), custom_call_target="tpu_custom_call" | custom-call | tf_op jit(solution)/shard_map/exchange/pallas_call | solution.py:547
  24.1 1.4 %third.1 = f32[192,2048]{1,0:T(8,128)} custom-call(f32[192,2048]{1,0:T(8,128)S(1)} %exchange.1.x_ref), custom_call_target="tpu_custom_call" | custom-call | tf_op jit(solution)/shard_map/third/pallas_call | solution.py:575

commit v5 on v4

--- a/solution.py
+++ b/solution.py
@@ -290,7 +290,6 @@
             send_x(0, 2)
             send_y(0, 2)
             send_y(1, 2)
-            send_x(1, 2)
 
         @pl.when(i == 2)
         def _():
@@ -427,12 +426,12 @@
             def _(s=s, r=r):
                 across(s, r).start()
 
+    send_x(1, 2)
+
     send_x(0, 0)
 
     send_y(0, 0)
     send_y(1, 0)
-
-    send_x(1, 0)
 
     for r in (1, 0):
 
@@ -449,6 +448,8 @@
             along_y(0, r, passed.at[3 * r + 2]).start()
 
     send_x(0, 3)
+
+    send_x(1, 0)
 
     send_y(0, 3)
     send_y(1, 3)

time: 25.7 us -> 25.5 us (level)
  the two profiles are of different devices: /device:TPU:220 before, /device:TPU:204 now
where the time goes in v5:
time: 25.5 us; the launch traced here: 25.4 us
  Pallas kernels  25.3 us (99%)
    pallas_call x1, Pallas kernels, local(): pl.pallas_call(functools.partial(exchange_kernel, sizes), name='exchange'...  23.9 us
    pallas_call x1, Pallas kernels, local(): pl.pallas_call(third_direction_kernel, name='third', out_shape=jax.ShapeD...  1.42 us

profile of v5, /device:TPU:204, one launch (start us, length us, event | category | flops | bytes accessed | tf_op | source)
XLA Modules:
  0.0 25.4 jit_solution(1003800231724974874)
XLA Ops:
  0.0 23.9 %exchange.1.x_ref = f32[192,2048]{1,0:T(8,128)S(1)} custom-call(f32[192,2048]{1,0:T(8,128)} %bitcast.2, f32[6,1,1,256]{3,2,1,0:T(1,128)} %g_hbm.1, bf16[2,256,256]{2,1,0:T(8,128)(2,1)} %constant.2.clone.tables_hbm), custom_call_target="tpu_custom_call" | custom-call | tf_op jit(solution)/shard_map/exchange/pallas_call | solution.py:548
  23.9 1.4 %third.1 = f32[192,2048]{1,0:T(8,128)} custom-call(f32[192,2048]{1,0:T(8,128)S(1)} %exchange.1.x_ref), custom_call_target="tpu_custom_call" | custom-call | tf_op jit(solution)/shard_map/third/pallas_call | solution.py:576
